TPU v7x, 32 devices: a whole 2x2x4 slice. The times are simulated.
32 devices in a mesh: space: 8 (over z, y), slab: 4 (over x, core).
Axes of the slice: x: 2, y: 2, z: 4, core: 2. Of those that a mesh axis runs over, the one named last changes fastest.
Arguments:
- source: float32 [4, 256, 2048], P('slab', None, 'space'), may hold values from -6 to 6
- initial: float32 [64, 2048], P(None, 'space'), may hold values from -6 to 6
- inverse: float32 [256, 256], replicated, may hold values from -0.1 to 0.7, as said below
- lift: float32 [256, 384], replicated, may hold values from -0.109375 to 0.109375
- lift_time: float32 [256, 64], replicated, may hold values from -0.375 to 0.375
- links: int32 [6, 2048], P(None, 'space'), may hold values from 0 to 1791, as said below
- orient: int32 [6, 2048], P(None, 'space'), may hold values from 0 to 7
- exports: int32 [2048], P('space'), may hold values from 0 to 1535, as said below
- counts: int32 [8], P('space'), may hold values from 128 to 256, as said below
Outputs:
- state: float32 [4, 256, 2048], P('slab', None, 'space')
Inputs may be any that keep to these rules, and one draw needn't show every extreme that they name: `links`: a value below 1536 is f*256 + e naming face f of a live slot e of the same partition; others are 1536 + m naming slot m of the imported neighbour traces. `exports`: each value is f*256 + e with e a live slot of that partition. `counts`: some partition holds exactly 256. `inverse`: full rank; diagonal entries between 0.5 and 0.7, off-diagonal entries of magnitude at most 0.1.
All inputs are finite; a program needn't handle non-finite values.
Results may differ from a plain program's by a relative error of at most 0.0001.
Values sent between devices are 32-bit elements; how exact they have to be, the bound alone decides.
No kernel may reach another device: no remote copies, remote signals or barrier semaphores. Data moves between devices by JAX's collectives and lax.ppermute only.
A program may use at most 64 MiB of HBM per device.

v0:
```python
import jax
import jax.numpy as jnp
from jax import lax
from jax.sharding import PartitionSpec as P

ITERS = 6


def with_halo(block, sides, width):
    for axis, dim in sides:
        count = lax.axis_size(axis)
        forward = [(i, i + 1) for i in range(count - 1)]
        forward.append((count - 1, 0))
        backward = [(target, source) for source, target in forward]
        low = lax.ppermute(
            lax.slice_in_dim(block, block.shape[dim] - width, None, axis=dim), axis, forward
        )
        high = lax.ppermute(lax.slice_in_dim(block, 0, width, axis=dim), axis, backward)
        block = jnp.concatenate([low, block, high], axis=dim)
    return block


def shifted(block, axis, distance):
    devices = range(lax.axis_size(axis))
    route = [(i - distance, i) for i in devices if i - distance in devices]
    return lax.ppermute(block, axis, route)


def face_stack(volume, axis):
    pieces = [
        volume[:, 0],
        volume[:, 3],
        volume[:, :, 0],
        volume[:, :, 3],
        volume[:, :, :, 0],
        volume[:, :, :, 3],
    ]
    return jnp.stack(pieces, axis=axis)


def orient_traces(values, turn):
    swapped = jnp.swapaxes(values, 1, 2)
    values = jnp.where(jnp.bitwise_and(turn, 4) > 0, swapped, values)
    values = jnp.where(jnp.bitwise_and(turn, 1) > 0, jnp.flip(values, 1), values)
    values = jnp.where(jnp.bitwise_and(turn, 2) > 0, jnp.flip(values, 2), values)
    return values


def body(source, initial, inverse, lift, lift_time, links, orient, exports, counts):
    highest = lax.Precision.HIGHEST
    elems = links.shape[1]
    peer = exports.shape[0] // 2
    local_width = 6 * elems
    live = (jnp.arange(elems, dtype=jnp.int32) < counts[0]).astype(jnp.float32)[None, :]
    flat_links = links.reshape(-1)
    first_slab = lax.axis_index("slab") == 0
    state = jnp.zeros((256, elems), jnp.float32)
    for step in range(ITERS):
        traces = face_stack(state.reshape(4, 4, 4, 4, elems), 3).reshape(64, local_width)
        outgoing = jnp.take(traces, exports, axis=1)
        extended = with_halo(outgoing, (("space", 1),), peer)
        table = jnp.concatenate([traces, extended[:, :peer], extended[:, 3 * peer :]], axis=1)
        gathered = jnp.take(table, flat_links, axis=1)
        nbr = orient_traces(gathered.reshape(4, 4, 4, 6, elems), orient).reshape(384, elems)
        top = state[192:]
        arrived = shifted(top, "slab", 1)
        top_in = jnp.where(first_slab, initial, arrived)
        time_term = jnp.dot(lift_time, top_in, precision=highest)
        rhs = source[0] + jnp.dot(lift, nbr, precision=highest) + time_term
        state = jnp.dot(inverse, rhs, precision=highest) * live
    return state[None]


def solution(mesh):
    return jax.shard_map(
        body,
        mesh=mesh,
        in_specs=(
            P("slab", None, "space"),
            P(None, "space"),
            P(),
            P(),
            P(),
            P(None, "space"),
            P(None, "space"),
            P("space"),
            P("space"),
        ),
        out_specs=P("slab", None, "space"),
        check_vma=False,
    )
```

profile of v0, /device:TPU:0, one launch (start us, length us, event | category | flops | bytes accessed | tf_op | source)
XLA Modules:
  0.0 92.6 jit_solution(5732063632681816826)
XLA Ops:
  0.0 2.5 %collective-permute-start.2 = (f32[64,256]{1,0:T(8,128)S(1)}, f32[64,256]{1,0:T(8,128)S(1)}, u32[]{:S(2)}, u32[]{:S(2)}) collective-permute-start(f32[64,256]{1,0:T(8,128)S(1)} %slice.146), channel_id=1, source_target_pairs={{0,1},{1,2},{2,3},{4,5},{5,6},{6,7},{8,9},{9,10},{10,11},{12,13},{... | collective-permute-start | bytes 196616 | tf_op jit(solution)/shard_map/ppermute | solution.py:26
  3.8 2.4 %collective-permute-start = (f32[64,128]{0,1:T(8,128)S(1)}, f32[64,128]{0,1:T(8,128)S(1)}, u32[]{:S(2)}, u32[]{:S(2)}) collective-permute-start(f32[64,128]{0,1:T(8,128)S(1)} %get-tuple-element.47), channel_id=1, source_target_pairs={{0,4},{4,8},{8,12},{12,16},{16,20},{20,24},{24,28},{28,0},{1,5},{5... | collective-permute-start | bytes 98312 | tf_op jit(solution)/shard_map/ppermute | solution.py:15
  6.2 3.1 %collective-permute-start.1 = (f32[64,128]{0,1:T(8,128)S(1)}, f32[64,128]{0,1:T(8,128)S(1)}, u32[]{:S(2)}, u32[]{:S(2)}) collective-permute-start(f32[64,128]{0,1:T(8,128)S(1)} %get-tuple-element.48), channel_id=1, source_target_pairs={{4,0},{8,4},{12,8},{16,12},{20,16},{24,20},{28,24},{0,28},{5,1},{9... | collective-permute-start | bytes 98312 | tf_op jit(solution)/shard_map/ppermute | solution.py:18
  10.1 1.5 %collective-permute-done = f32[64,128]{0,1:T(8,128)S(1)} collective-permute-done((f32[64,128]{0,1:T(8,128)S(1)}, f32[64,128]{0,1:T(8,128)S(1)}, u32[]{:S(2)}, u32[]{:S(2)}) %collective-permute-start) | collective-permute-done | bytes 32800 | tf_op jit(solution)/shard_map/ppermute | solution.py:15
  11.7 2.6 %gather_fusion.1 = f32[1536,64]{1,0:T(8,128)S(1)} fusion(f32[64,1792]{0,1:T(8,128)S(1)} %pad_maximum_fusion, s32[2048]{0:T(1024)S(1)} %pad_clamp_fusion), kind=kCustom, calls=%fused_computation.1.clone | custom fusion | bytes 792576 | tf_op jit(solution)/shard_map/jit(_take)/gather | solution.py:63
  15.2 0.9 copy-done.1
  20.5 1.5 %collective-permute-start.3 = (f32[64,128]{0,1:T(8,128)S(1)}, f32[64,128]{0,1:T(8,128)S(1)}, u32[]{:S(2)}, u32[]{:S(2)}) collective-permute-start(f32[64,128]{0,1:T(8,128)S(1)} %get-tuple-element.45), channel_id=1, source_target_pairs={{0,4},{4,8},{8,12},{12,16},{16,20},{20,24},{24,28},{28,0},{1,5},{5... | collective-permute-start | bytes 98312 | tf_op jit(solution)/shard_map/ppermute | solution.py:15
  22.0 3.3 %collective-permute-start.4 = (f32[64,128]{0,1:T(8,128)S(1)}, f32[64,128]{0,1:T(8,128)S(1)}, u32[]{:S(2)}, u32[]{:S(2)}) collective-permute-start(f32[64,128]{0,1:T(8,128)S(1)} %get-tuple-element.46), channel_id=1, source_target_pairs={{4,0},{8,4},{12,8},{16,12},{20,16},{24,20},{28,24},{0,28},{5,1},{9... | collective-permute-start | bytes 98312 | tf_op jit(solution)/shard_map/ppermute | solution.py:18
  25.3 2.2 %collective-permute-start.5 = (f32[64,256]{1,0:T(8,128)S(1)}, f32[64,256]{1,0:T(8,128)S(1)}, u32[]{:S(2)}, u32[]{:S(2)}) collective-permute-start(f32[64,256]{1,0:T(8,128)S(1)} %slice.226), channel_id=1, source_target_pairs={{0,1},{1,2},{2,3},{4,5},{5,6},{6,7},{8,9},{9,10},{10,11},{12,13},{... | collective-permute-start | bytes 196616 | tf_op jit(solution)/shard_map/ppermute | solution.py:26
  28.2 2.6 %gather_fusion.3 = f32[1536,64]{1,0:T(8,128)S(1)} fusion(f32[64,1792]{0,1:T(8,128)S(1)} %pad_maximum_fusion.1, s32[2048]{0:T(1024)S(1)} %pad_clamp_fusion), kind=kCustom, calls=%fused_computation.7.clone | custom fusion | bytes 792576 | tf_op jit(solution)/shard_map/jit(_take)/gather | solution.py:63
  35.5 1.0 %collective-permute-start.6 = (f32[64,128]{0,1:T(8,128)S(1)}, f32[64,128]{0,1:T(8,128)S(1)}, u32[]{:S(2)}, u32[]{:S(2)}) collective-permute-start(f32[64,128]{0,1:T(8,128)S(1)} %get-tuple-element.43), channel_id=1, source_target_pairs={{0,4},{4,8},{8,12},{12,16},{16,20},{20,24},{24,28},{28,0},{1,5},{5... | collective-permute-start | bytes 98312 | tf_op jit(solution)/shard_map/ppermute | solution.py:15
  36.5 3.8 %collective-permute-start.7 = (f32[64,128]{0,1:T(8,128)S(1)}, f32[64,128]{0,1:T(8,128)S(1)}, u32[]{:S(2)}, u32[]{:S(2)}) collective-permute-start(f32[64,128]{0,1:T(8,128)S(1)} %get-tuple-element.44), channel_id=1, source_target_pairs={{4,0},{8,4},{12,8},{16,12},{20,16},{24,20},{28,24},{0,28},{5,1},{9... | collective-permute-start | bytes 98312 | tf_op jit(solution)/shard_map/ppermute | solution.py:18
  40.3 2.5 %collective-permute-start.8 = (f32[64,256]{1,0:T(8,128)S(1)}, f32[64,256]{1,0:T(8,128)S(1)}, u32[]{:S(2)}, u32[]{:S(2)}) collective-permute-start(f32[64,256]{1,0:T(8,128)S(1)} %slice.235), channel_id=1, source_target_pairs={{0,1},{1,2},{2,3},{4,5},{5,6},{6,7},{8,9},{9,10},{10,11},{12,13},{... | collective-permute-start | bytes 196616 | tf_op jit(solution)/shard_map/ppermute | solution.py:26
  43.3 2.6 %gather_fusion.5 = f32[1536,64]{1,0:T(8,128)S(1)} fusion(f32[64,1792]{0,1:T(8,128)S(1)} %pad_maximum_fusion.2, s32[2048]{0:T(1024)S(1)} %pad_clamp_fusion), kind=kCustom, calls=%fused_computation.8.clone | custom fusion | bytes 792576 | tf_op jit(solution)/shard_map/jit(_take)/gather | solution.py:63
  50.7 4.7 %collective-permute-start.10 = (f32[64,128]{0,1:T(8,128)S(1)}, f32[64,128]{0,1:T(8,128)S(1)}, u32[]{:S(2)}, u32[]{:S(2)}) collective-permute-start(f32[64,128]{0,1:T(8,128)S(1)} %get-tuple-element.42), channel_id=1, source_target_pairs={{4,0},{8,4},{12,8},{16,12},{20,16},{24,20},{28,24},{0,28},{5,1},{9... | collective-permute-start | bytes 98312 | tf_op jit(solution)/shard_map/ppermute | solution.py:18
  55.4 1.9 %collective-permute-start.11 = (f32[64,256]{1,0:T(8,128)S(1)}, f32[64,256]{1,0:T(8,128)S(1)}, u32[]{:S(2)}, u32[]{:S(2)}) collective-permute-start(f32[64,256]{1,0:T(8,128)S(1)} %slice.244), channel_id=1, source_target_pairs={{0,1},{1,2},{2,3},{4,5},{5,6},{6,7},{8,9},{9,10},{10,11},{12,13},{... | collective-permute-start | bytes 196616 | tf_op jit(solution)/shard_map/ppermute | solution.py:26
  58.0 2.6 %gather_fusion.7 = f32[1536,64]{1,0:T(8,128)S(1)} fusion(f32[64,1792]{0,1:T(8,128)S(1)} %pad_maximum_fusion.3, s32[2048]{0:T(1024)S(1)} %pad_clamp_fusion), kind=kCustom, calls=%fused_computation.9.clone | custom fusion | bytes 792576 | tf_op jit(solution)/shard_map/jit(_take)/gather | solution.py:63
  65.5 4.7 %collective-permute-start.13 = (f32[64,128]{0,1:T(8,128)S(1)}, f32[64,128]{0,1:T(8,128)S(1)}, u32[]{:S(2)}, u32[]{:S(2)}) collective-permute-start(f32[64,128]{0,1:T(8,128)S(1)} %get-tuple-element.40), channel_id=1, source_target_pairs={{4,0},{8,4},{12,8},{16,12},{20,16},{24,20},{28,24},{0,28},{5,1},{9... | collective-permute-start | bytes 98312 | tf_op jit(solution)/shard_map/ppermute | solution.py:18
  70.2 1.5 %collective-permute-start.14 = (f32[64,256]{1,0:T(8,128)S(1)}, f32[64,256]{1,0:T(8,128)S(1)}, u32[]{:S(2)}, u32[]{:S(2)}) collective-permute-start(f32[64,256]{1,0:T(8,128)S(1)} %slice.253), channel_id=1, source_target_pairs={{0,1},{1,2},{2,3},{4,5},{5,6},{6,7},{8,9},{9,10},{10,11},{12,13},{... | collective-permute-start | bytes 196616 | tf_op jit(solution)/shard_map/ppermute | solution.py:26
  72.5 2.6 %gather_fusion.9 = f32[1536,64]{1,0:T(8,128)S(1)} fusion(f32[64,1792]{0,1:T(8,128)S(1)} %pad_maximum_fusion.4, s32[2048]{0:T(1024)S(1)} %pad_clamp_fusion), kind=kCustom, calls=%fused_computation.10.clone | custom fusion | bytes 792576 | tf_op jit(solution)/shard_map/jit(_take)/gather | solution.py:63
  79.9 4.8 %collective-permute-start.16 = (f32[64,128]{0,1:T(8,128)S(1)}, f32[64,128]{0,1:T(8,128)S(1)}, u32[]{:S(2)}, u32[]{:S(2)}) collective-permute-start(f32[64,128]{0,1:T(8,128)S(1)} %get-tuple-element.38), channel_id=1, source_target_pairs={{4,0},{8,4},{12,8},{16,12},{20,16},{24,20},{28,24},{0,28},{5,1},{9... | collective-permute-start | bytes 98312 | tf_op jit(solution)/shard_map/ppermute | solution.py:18
  84.7 1.5 %collective-permute-start.17 = (f32[64,256]{1,0:T(8,128)S(1)}, f32[64,256]{1,0:T(8,128)S(1)}, u32[]{:S(2)}, u32[]{:S(2)}) collective-permute-start(f32[64,256]{1,0:T(8,128)S(1)} %slice.262), channel_id=1, source_target_pairs={{0,1},{1,2},{2,3},{4,5},{5,6},{6,7},{8,9},{9,10},{10,11},{12,13},{... | collective-permute-start | bytes 196616 | tf_op jit(solution)/shard_map/ppermute | solution.py:26
  86.9 2.6 %gather_fusion.11 = f32[1536,64]{1,0:T(8,128)S(1)} fusion(f32[64,1792]{0,1:T(8,128)S(1)} %pad_maximum_fusion.5, s32[2048]{0:T(1024)S(1)} %pad_clamp_fusion), kind=kCustom, calls=%fused_computation.11.clone | custom fusion | bytes 792576 | tf_op jit(solution)/shard_map/jit(_take)/gather | solution.py:63
  91.5 1.1 %fusion = f32[1,256,256]{2,1,0:T(8,128)} fusion(f32[256,256]{1,0:T(8,128)S(1)} %fusion.12, f32[256,256]{1,0:T(8,128)S(1)} %copy-done.2, f32[256]{0:T(256)S(1)} %compare_convert_fusion), kind=kOutput, calls=%fused_computation.13 | convolution fusion | flops 201392128 | bytes 787456 | tf_op jit(solution)/shard_map/dot_general | solution.py:70
  (193 shorter events, 30.1 us)
Async XLA Ops:
  0.0 15.2 %copy-start = (f32[256,384]{1,0:T(8,128)S(1)}, f32[256,384]{1,0:T(8,128)}, u32[]{:S(2)}) copy-start(f32[256,384]{1,0:T(8,128)} %param.16) | copy-start | bytes 1179652
  0.0 2.6 %copy-start.7 = (s32[256]{0:T(256)S(1)}, s32[256]{0:T(256)}, u32[]{:S(2)}) copy-start(s32[256]{0:T(256)} %param.20) | copy-start | bytes 3076
  0.0 16.7 %collective-permute-start.2 = (f32[64,256]{1,0:T(8,128)S(1)}, f32[64,256]{1,0:T(8,128)S(1)}, u32[]{:S(2)}, u32[]{:S(2)}) collective-permute-start(f32[64,256]{1,0:T(8,128)S(1)} %slice.146), channel_id=1, source_target_pairs={{0,1},{1,2},{2,3},{4,5},{5,6},{6,7},{8,9},{9,10},{10,11},{12,13},{... | collective-permute-start | bytes 196616 | tf_op jit(solution)/shard_map/ppermute | solution.py:26
  3.8 5.5 %copy-start.6 = (s32[6,256]{1,0:T(8,128)S(1)}, s32[6,256]{1,0:T(8,128)}, u32[]{:S(2)}) copy-start(s32[6,256]{1,0:T(8,128)} %param.18) | copy-start | bytes 18436
  3.8 7.8 %collective-permute-start = (f32[64,128]{0,1:T(8,128)S(1)}, f32[64,128]{0,1:T(8,128)S(1)}, u32[]{:S(2)}, u32[]{:S(2)}) collective-permute-start(f32[64,128]{0,1:T(8,128)S(1)} %get-tuple-element.47), channel_id=1, source_target_pairs={{0,4},{4,8},{8,12},{12,16},{16,20},{20,24},{24,28},{28,0},{1,5},{5... | collective-permute-start | bytes 98312 | tf_op jit(solution)/shard_map/ppermute | solution.py:15
  6.2 5.4 %collective-permute-start.1 = (f32[64,128]{0,1:T(8,128)S(1)}, f32[64,128]{0,1:T(8,128)S(1)}, u32[]{:S(2)}, u32[]{:S(2)}) collective-permute-start(f32[64,128]{0,1:T(8,128)S(1)} %get-tuple-element.48), channel_id=1, source_target_pairs={{4,0},{8,4},{12,8},{16,12},{20,16},{24,20},{28,24},{0,28},{5,1},{9... | collective-permute-start | bytes 98312 | tf_op jit(solution)/shard_map/ppermute | solution.py:18
  15.1 1.0 %copy-start.1 = (f32[1,256,256]{2,1,0:T(8,128)S(1)}, f32[1,256,256]{2,1,0:T(8,128)}, u32[]{:S(2)}) copy-start(f32[1,256,256]{2,1,0:T(8,128)} %param.13) | copy-start | bytes 786436
  16.0 0.9 copy-start.4
  16.7 1.0 %copy-start.2 = (f32[256,256]{1,0:T(8,128)S(1)}, f32[256,256]{1,0:T(8,128)}, u32[]{:S(2)}) copy-start(f32[256,256]{1,0:T(8,128)} %param.15) | copy-start | bytes 786436
  20.5 7.6 %collective-permute-start.3 = (f32[64,128]{0,1:T(8,128)S(1)}, f32[64,128]{0,1:T(8,128)S(1)}, u32[]{:S(2)}, u32[]{:S(2)}) collective-permute-start(f32[64,128]{0,1:T(8,128)S(1)} %get-tuple-element.45), channel_id=1, source_target_pairs={{0,4},{4,8},{8,12},{12,16},{16,20},{20,24},{24,28},{28,0},{1,5},{5... | collective-permute-start | bytes 98312 | tf_op jit(solution)/shard_map/ppermute | solution.py:15
  22.0 6.1 %collective-permute-start.4 = (f32[64,128]{0,1:T(8,128)S(1)}, f32[64,128]{0,1:T(8,128)S(1)}, u32[]{:S(2)}, u32[]{:S(2)}) collective-permute-start(f32[64,128]{0,1:T(8,128)S(1)} %get-tuple-element.46), channel_id=1, source_target_pairs={{4,0},{8,4},{12,8},{16,12},{20,16},{24,20},{28,24},{0,28},{5,1},{9... | collective-permute-start | bytes 98312 | tf_op jit(solution)/shard_map/ppermute | solution.py:18
  25.3 7.0 %collective-permute-start.5 = (f32[64,256]{1,0:T(8,128)S(1)}, f32[64,256]{1,0:T(8,128)S(1)}, u32[]{:S(2)}, u32[]{:S(2)}) collective-permute-start(f32[64,256]{1,0:T(8,128)S(1)} %slice.226), channel_id=1, source_target_pairs={{0,1},{1,2},{2,3},{4,5},{5,6},{6,7},{8,9},{9,10},{10,11},{12,13},{... | collective-permute-start | bytes 196616 | tf_op jit(solution)/shard_map/ppermute | solution.py:26
  35.5 7.7 %collective-permute-start.6 = (f32[64,128]{0,1:T(8,128)S(1)}, f32[64,128]{0,1:T(8,128)S(1)}, u32[]{:S(2)}, u32[]{:S(2)}) collective-permute-start(f32[64,128]{0,1:T(8,128)S(1)} %get-tuple-element.43), channel_id=1, source_target_pairs={{0,4},{4,8},{8,12},{12,16},{16,20},{20,24},{24,28},{28,0},{1,5},{5... | collective-permute-start | bytes 98312 | tf_op jit(solution)/shard_map/ppermute | solution.py:15
  36.5 6.7 %collective-permute-start.7 = (f32[64,128]{0,1:T(8,128)S(1)}, f32[64,128]{0,1:T(8,128)S(1)}, u32[]{:S(2)}, u32[]{:S(2)}) collective-permute-start(f32[64,128]{0,1:T(8,128)S(1)} %get-tuple-element.44), channel_id=1, source_target_pairs={{4,0},{8,4},{12,8},{16,12},{20,16},{24,20},{28,24},{0,28},{5,1},{9... | collective-permute-start | bytes 98312 | tf_op jit(solution)/shard_map/ppermute | solution.py:18
  40.3 7.1 %collective-permute-start.8 = (f32[64,256]{1,0:T(8,128)S(1)}, f32[64,256]{1,0:T(8,128)S(1)}, u32[]{:S(2)}, u32[]{:S(2)}) collective-permute-start(f32[64,256]{1,0:T(8,128)S(1)} %slice.235), channel_id=1, source_target_pairs={{0,1},{1,2},{2,3},{4,5},{5,6},{6,7},{8,9},{9,10},{10,11},{12,13},{... | collective-permute-start | bytes 196616 | tf_op jit(solution)/shard_map/ppermute | solution.py:26
  50.6 7.3 %collective-permute-start.9 = (f32[64,128]{0,1:T(8,128)S(1)}, f32[64,128]{0,1:T(8,128)S(1)}, u32[]{:S(2)}, u32[]{:S(2)}) collective-permute-start(f32[64,128]{0,1:T(8,128)S(1)} %get-tuple-element.41), channel_id=1, source_target_pairs={{0,4},{4,8},{8,12},{12,16},{16,20},{20,24},{24,28},{28,0},{1,5},{5... | collective-permute-start | bytes 98312 | tf_op jit(solution)/shard_map/ppermute | solution.py:15
  50.7 7.3 %collective-permute-start.10 = (f32[64,128]{0,1:T(8,128)S(1)}, f32[64,128]{0,1:T(8,128)S(1)}, u32[]{:S(2)}, u32[]{:S(2)}) collective-permute-start(f32[64,128]{0,1:T(8,128)S(1)} %get-tuple-element.42), channel_id=1, source_target_pairs={{4,0},{8,4},{12,8},{16,12},{20,16},{24,20},{28,24},{0,28},{5,1},{9... | collective-permute-start | bytes 98312 | tf_op jit(solution)/shard_map/ppermute | solution.py:18
  55.4 6.7 %collective-permute-start.11 = (f32[64,256]{1,0:T(8,128)S(1)}, f32[64,256]{1,0:T(8,128)S(1)}, u32[]{:S(2)}, u32[]{:S(2)}) collective-permute-start(f32[64,256]{1,0:T(8,128)S(1)} %slice.244), channel_id=1, source_target_pairs={{0,1},{1,2},{2,3},{4,5},{5,6},{6,7},{8,9},{9,10},{10,11},{12,13},{... | collective-permute-start | bytes 196616 | tf_op jit(solution)/shard_map/ppermute | solution.py:26
  65.4 7.0 %collective-permute-start.12 = (f32[64,128]{0,1:T(8,128)S(1)}, f32[64,128]{0,1:T(8,128)S(1)}, u32[]{:S(2)}, u32[]{:S(2)}) collective-permute-start(f32[64,128]{0,1:T(8,128)S(1)} %get-tuple-element.39), channel_id=1, source_target_pairs={{0,4},{4,8},{8,12},{12,16},{16,20},{20,24},{24,28},{28,0},{1,5},{5... | collective-permute-start | bytes 98312 | tf_op jit(solution)/shard_map/ppermute | solution.py:15
  65.5 7.0 %collective-permute-start.13 = (f32[64,128]{0,1:T(8,128)S(1)}, f32[64,128]{0,1:T(8,128)S(1)}, u32[]{:S(2)}, u32[]{:S(2)}) collective-permute-start(f32[64,128]{0,1:T(8,128)S(1)} %get-tuple-element.40), channel_id=1, source_target_pairs={{4,0},{8,4},{12,8},{16,12},{20,16},{24,20},{28,24},{0,28},{5,1},{9... | collective-permute-start | bytes 98312 | tf_op jit(solution)/shard_map/ppermute | solution.py:18
  70.2 6.4 %collective-permute-start.14 = (f32[64,256]{1,0:T(8,128)S(1)}, f32[64,256]{1,0:T(8,128)S(1)}, u32[]{:S(2)}, u32[]{:S(2)}) collective-permute-start(f32[64,256]{1,0:T(8,128)S(1)} %slice.253), channel_id=1, source_target_pairs={{0,1},{1,2},{2,3},{4,5},{5,6},{6,7},{8,9},{9,10},{10,11},{12,13},{... | collective-permute-start | bytes 196616 | tf_op jit(solution)/shard_map/ppermute | solution.py:26
  79.9 7.0 %collective-permute-start.15 = (f32[64,128]{0,1:T(8,128)S(1)}, f32[64,128]{0,1:T(8,128)S(1)}, u32[]{:S(2)}, u32[]{:S(2)}) collective-permute-start(f32[64,128]{0,1:T(8,128)S(1)} %get-tuple-element.37), channel_id=1, source_target_pairs={{0,4},{4,8},{8,12},{12,16},{16,20},{20,24},{24,28},{28,0},{1,5},{5... | collective-permute-start | bytes 98312 | tf_op jit(solution)/shard_map/ppermute | solution.py:15
  79.9 7.0 %collective-permute-start.16 = (f32[64,128]{0,1:T(8,128)S(1)}, f32[64,128]{0,1:T(8,128)S(1)}, u32[]{:S(2)}, u32[]{:S(2)}) collective-permute-start(f32[64,128]{0,1:T(8,128)S(1)} %get-tuple-element.38), channel_id=1, source_target_pairs={{4,0},{8,4},{12,8},{16,12},{20,16},{24,20},{28,24},{0,28},{5,1},{9... | collective-permute-start | bytes 98312 | tf_op jit(solution)/shard_map/ppermute | solution.py:18
  84.7 6.3 %collective-permute-start.17 = (f32[64,256]{1,0:T(8,128)S(1)}, f32[64,256]{1,0:T(8,128)S(1)}, u32[]{:S(2)}, u32[]{:S(2)}) collective-permute-start(f32[64,256]{1,0:T(8,128)S(1)} %slice.262), channel_id=1, source_target_pairs={{0,1},{1,2},{2,3},{4,5},{5,6},{6,7},{8,9},{9,10},{10,11},{12,13},{... | collective-permute-start | bytes 196616 | tf_op jit(solution)/shard_map/ppermute | solution.py:26
  (2 other events, 1.5 us)
where the time goes:
time: 92.9 us; the launch traced here: 92.6 us
  starting transfers between devices  41.6 us (45%)
  local copies, waits for them, and re-layouts  31.9 us (34%)
  matrix products  9.2 us (10%)
  waiting for transfers between devices  4.57 us (5%)
  other arithmetic  3.37 us (4%)
  between operations  1.98 us (2%)
    ppermute x6, starting transfers between devices, with_halo(): lax.ppermute(lax.slice_in_dim(block, 0, width, axis=dim), axis, backward)  24.4 us
    gather x6, local copies, waits for them, and re-layouts, body(): gathered = jnp.take(table, flat_links, axis=1)  15.6 us
    ppermute x6, starting transfers between devices, shifted(): return lax.ppermute(block, axis, route)  12.1 us
    ppermute x6, starting transfers between devices, with_halo(): lax.ppermute(lax.slice_in_dim(block, block.shape[dim] - width, None, axis...  5.04 us
    another operation x40, local copies, waits for them, and re-layouts, face_stack(): return jnp.stack(pieces, axis=axis)  5.04 us
    ppermute x6, waiting for transfers between devices, with_halo(): lax.ppermute(lax.slice_in_dim(block, block.shape[dim] - width, None, axis...  4.54 us
    gather x6, local copies, waits for them, and re-layouts, body(): outgoing = jnp.take(traces, exports, axis=1)  4.41 us
    dot_general x6, matrix products, body(): rhs = source[0] + jnp.dot(lift, nbr, precision=highest) + time_term  3.58 us
  transfers between devices with their start and end apart: 18, of which 6 were waited for; matrix products, arithmetic and copies ran while one was open for 28% of the time, Pallas kernels for 0%

commit v1 on v0

v1 whole, which is shorter than its diff:
```python
import jax
import jax.numpy as jnp
from jax import lax
from jax.experimental import pallas as pl
from jax.experimental.pallas import tpu as pltpu
from jax.sharding import PartitionSpec as P

ITERS = 6
F32 = jnp.float32
BF16 = jnp.bfloat16

VMEM = pl.BlockSpec(memory_space=pltpu.VMEM)
SMEM = pl.BlockSpec(memory_space=pltpu.SMEM)


def mm(a, b):
    return jnp.dot(a, b, preferred_element_type=F32)


def split(x):
    hi = x.astype(BF16)
    return hi, (x - hi.astype(F32)).astype(BF16)


def iota(shape, dim):
    return lax.broadcasted_iota(jnp.int32, shape, dim)


def one_hot(hit):
    return jnp.where(hit, 1.0, 0.0).astype(BF16)


def halves(x):
    hi = x.astype(BF16).astype(F32)
    return jnp.where(iota(x.shape, 0) % 8 < 4, hi, x - hi)


def face_node(face, a, b):
    end = 3 * (face % 2)
    if face < 2:
        return end * 16 + a * 4 + b
    if face < 4:
        return a * 16 + end * 4 + b
    return a * 16 + b * 4 + end


def publish(rows, rows_ref, exports, table_ref, top_ref, low_ref, high_ref):
    elems = rows.shape[1]
    peer = low_ref.shape[1]
    for c in range(rows_ref.shape[0]):
        rows_ref[c] = rows[:, c * 128 : (c + 1) * 128]
        top_ref[:, c * 128 : (c + 1) * 128] = rows_ref[c, pl.ds(3, 64, stride=8), :]
    parts = halves(rows)
    sent = None
    for face in range(6):
        piece = jnp.concatenate(
            [parts[8 * face_node(face, a, b) :][:8] for a in range(4) for b in range(4)], axis=0
        ).astype(BF16)
        table_ref[:, face * elems : (face + 1) * elems] = piece
    pick = one_hot(iota((6 * elems, 2 * peer), 0) == exports)
    sent = mm(table_ref[...], pick)
    first = iota((8, 2 * peer), 0) < 4
    for m in range(8):
        even = sent[16 * m : 16 * m + 8]
        odd = sent[16 * m + 8 : 16 * m + 16]
        even = even + pltpu.roll(even, 4, 0)
        odd = odd + pltpu.roll(odd, 4, 0)
        both = jnp.where(first, even, odd)
        low_ref[8 * m : 8 * m + 8, :] = both[:, :peer]
        high_ref[8 * m : 8 * m + 8, :] = both[:, peer:]


def live_of(counts_ref, elems):
    return jnp.where(iota((1, elems), 1) < counts_ref[0], 1.0, 0.0)


def prepare(counts, first, source, initial, inverse, lift, lift_time, exports,
            weight, base, table, top, low, high, rows_ref):
    elems = source.shape[2]
    dup = iota((512, 256), 0)
    row_pick = one_hot((dup % 4) * 64 + dup // 8 == iota((512, 256), 1))
    inv_hi, inv_lo = split(inverse[...])
    inv_hi = mm(row_pick, inv_hi).astype(BF16)
    inv_lo = mm(row_pick, inv_lo).astype(BF16)

    def solve(x_hi, x_lo):
        return mm(inv_hi, x_hi) + (mm(inv_hi, x_lo) + mm(inv_lo, x_hi))

    start = initial[...] * jnp.where(first[0] > 0, 1.0, 0.0)
    lt_hi, lt_lo = split(lift_time[...])
    st_hi, st_lo = split(start)
    rhs = source[0] + (mm(lt_hi, st_hi) + (mm(lt_hi, st_lo) + mm(lt_lo, st_hi)))
    rows = solve(*split(rhs)) * live_of(counts, elems)
    base[...] = rows
    publish(rows, rows_ref, exports[...], table, top, low, high)

    col = iota((384, 768), 1)
    want = ((col % 4) * 16 + (col // 8) % 16) * 6 + col // 128
    col_pick = one_hot(want == iota((384, 768), 0))
    l_hi, l_lo = split(lift[...])
    l_hi = mm(l_hi, col_pick).astype(BF16)
    l_lo = mm(l_lo, col_pick).astype(BF16)
    w_hi, w_lo = split(solve(l_hi, l_lo))
    weight[0:512, 0:768] = w_hi
    weight[512:1024, 0:768] = w_lo
    t_hi, t_lo = split(solve(jnp.concatenate([lt_hi, lt_hi], 1), jnp.concatenate([lt_lo, lt_lo], 1)))
    weight[0:512, 768:896] = t_hi
    weight[512:1024, 768:896] = t_lo


def gather_local(table, links, out):
    elems = links.shape[1] // 6
    for face in range(6):
        cols = slice(face * elems, (face + 1) * elems)
        pick = one_hot(iota((6 * elems, elems), 0) == links[:, cols])
        out[:, cols] = mm(table[...], pick).astype(BF16)


def advance(counts, local, from_low, from_high, top_in, weight, base, links, orient, nbr):
    elems = base.shape[1]
    peer = from_low.shape[1]
    first = iota((8, peer), 0) < 4
    sides = []
    for ref in (from_low, from_high):
        slabs = []
        for m in range(8):
            v = ref[8 * m : 8 * m + 8, :]
            r = pltpu.roll(v, 4, 0)
            slabs += [jnp.where(first, v, r), jnp.where(first, r, v)]
        sides.append(halves(jnp.concatenate(slabs, axis=0)).astype(BF16))
    imported = jnp.concatenate(sides, axis=1)
    for face in range(6):
        cols = slice(face * elems, (face + 1) * elems)
        pick = one_hot(iota((2 * peer, elems), 0) + 6 * elems == links[:, cols])
        got = local[:, cols].astype(F32) + mm(imported, pick)
        turn = jnp.broadcast_to(orient[:, cols], (8, elems))
        swap = (turn & 4) > 0
        rev_a = (turn & 1) > 0
        rev_b = (turn & 2) > 0
        v = [[got[8 * (a * 4 + b) :][:8] for b in range(4)] for a in range(4)]
        v = [[v[a][b] if a == b else jnp.where(swap, v[b][a], v[a][b]) for b in range(4)] for a in range(4)]
        v = [[jnp.where(rev_a, v[3 - a][b], v[a][b]) for b in range(4)] for a in range(4)]
        v = [[jnp.where(rev_b, v[a][3 - b], v[a][b]) for b in range(4)] for a in range(4)]
        nbr[face * 128 : (face + 1) * 128, :] = jnp.concatenate(sum(v, []), axis=0).astype(BF16)
    t_hi, t_lo = split(top_in[...])
    nbr[768:832, :] = t_hi
    nbr[832:896, :] = t_lo
    x = nbr[...]
    both = mm(weight[0:512, :], x) + mm(weight[512:1024, :], x)
    return (both + base[...]) * live_of(counts, elems)


def step_kernel(counts, local, from_low, from_high, top_in, weight, base, links, orient, exports,
                table, top, low, high, nbr, rows_ref):
    rows = advance(counts, local, from_low, from_high, top_in, weight, base, links, orient, nbr)
    publish(rows, rows_ref, exports[...], table, top, low, high)


def last_kernel(counts, local, from_low, from_high, top_in, weight, base, links, orient,
                out, nbr, rows_ref):
    rows = advance(counts, local, from_low, from_high, top_in, weight, base, links, orient, nbr)
    for c in range(rows_ref.shape[0]):
        rows_ref[c] = rows[:, c * 128 : (c + 1) * 128]
        for t in range(4):
            out[0, t * 64 : (t + 1) * 64, c * 128 : (c + 1) * 128] = rows_ref[c, pl.ds(t, 64, stride=8), :]


def body(source, initial, inverse, lift, lift_time, links, orient, exports, counts):
    elems = links.shape[1]
    peer = exports.shape[0] // 2
    links = links.reshape(1, 6 * elems)
    orient = orient.reshape(1, 6 * elems)
    exports = exports.reshape(1, 2 * peer)
    first = (lax.axis_index("slab") == 0).astype(jnp.int32).reshape(1)
    spaces = lax.axis_size("space")
    up = [(i, (i + 1) % spaces) for i in range(spaces)]
    down = [(b, a) for a, b in up]
    later = [(i, i + 1) for i in range(lax.axis_size("slab") - 1)]
    S = jax.ShapeDtypeStruct
    published = [
        S((128, 6 * elems), BF16),
        S((64, elems), F32),
        S((64, peer), F32),
        S((64, peer), F32),
    ]
    rows_scratch = pltpu.VMEM((elems // 128, 512, 128), F32)
    nbr_scratch = pltpu.VMEM((896, elems), BF16)

    weight, base, table, top, low, high = pl.pallas_call(
        prepare,
        out_shape=[S((1024, 896), BF16), S((512, elems), F32)] + published,
        in_specs=[SMEM, SMEM] + [VMEM] * 6,
        out_specs=[VMEM] * 6,
        scratch_shapes=[rows_scratch],
        name="prepare",
    )(counts, first, source, initial, inverse, lift, lift_time, exports)
    for step in range(1, ITERS):
        from_low = lax.ppermute(high, "space", up)
        from_high = lax.ppermute(low, "space", down)
        top_in = lax.ppermute(top, "slab", later)
        local = pl.pallas_call(
            gather_local,
            out_shape=S((128, 6 * elems), BF16),
            in_specs=[VMEM] * 2,
            out_specs=VMEM,
            name="gather_local",
        )(table, links)
        args = (counts, local, from_low, from_high, top_in, weight, base, links, orient)
        if step < ITERS - 1:
            table, top, low, high = pl.pallas_call(
                step_kernel,
                out_shape=published,
                in_specs=[SMEM] + [VMEM] * 9,
                out_specs=[VMEM] * 4,
                scratch_shapes=[nbr_scratch, rows_scratch],
                name="advance",
            )(*args, exports)
        else:
            out = pl.pallas_call(
                last_kernel,
                out_shape=S((1, 256, elems), F32),
                in_specs=[SMEM] + [VMEM] * 8,
                out_specs=VMEM,
                scratch_shapes=[nbr_scratch, rows_scratch],
                name="advance_last",
            )(*args)
    return out


def solution(mesh):
    return jax.shard_map(
        body,
        mesh=mesh,
        in_specs=(
            P("slab", None, "space"),
            P(None, "space"),
            P(),
            P(),
            P(),
            P(None, "space"),
            P(None, "space"),
            P("space"),
            P("space"),
        ),
        out_specs=P("slab", None, "space"),
        check_vma=False,
    )
```

time: 92.9 us -> 83.6 us (0.90)
  Pallas kernels: 0 us -> 36.5 us
  local copies, waits for them, and re-layouts: 31.9 us -> 9.68 us
  matrix products: 9.2 us -> 0 us
  starting transfers between devices: 41.6 us -> 35.9 us
  waiting for transfers between devices: 4.57 us -> 0.04 us
  other arithmetic: 3.37 us -> 0 us
  between operations: 1.98 us -> 0.85 us
    pallas_call x0 -> x11, Pallas kernels: none -> 36.5 us  [the longest x4 15.1 us: body(): pl.pallas_call(step_kernel, out_shape=published, in_specs=[SMEM] + [VMEM]...]
    gather x12 -> x0, local copies, waits for them, and re-layouts: 20 us -> none  [the longest x6 15.6 us: body(): gathered = jnp.take(table, flat_links, axis=1)]
    dot_general x18 -> x0, matrix products: 9.2 us -> none  [the longest x6 3.58 us: body(): rhs = source[0] + jnp.dot(lift, nbr, precision=highest) + time_term]
    unnamed x21 -> x33, local copies, waits for them, and re-layouts: 2.06 us -> 9.68 us
    ppermute x18 -> x15, starting transfers between devices: 41.6 us -> 35.9 us  [the longest x5 21.9 us: body(): from_high = lax.ppermute(low, 'space', down)]
    another operation x40 -> x0, local copies, waits for them, and re-layouts: 5.04 us -> none  [face_stack(): return jnp.stack(pieces, axis=axis)]
    ppermute x18 -> x15, waiting for transfers between devices: 4.57 us -> 0.04 us  [the longest x5 0.01 us: body(): from_low = lax.ppermute(high, 'space', up)]
    select_n x32 -> x0, other arithmetic: 2.95 us -> none  [the longest x7 1.61 us: body(): gathered = jnp.take(table, flat_links, axis=1)]
  transfers between devices with their start and end apart: 18 -> 15, of which waited for: 6 -> 0; matrix products, arithmetic and copies ran while one was open for 28% -> 3% of each run, Pallas kernels for 0% -> 15%
where the time goes in v1:
time: 83.6 us; the launch traced here: 83 us
  Pallas kernels  36.5 us (44%)
  starting transfers between devices  35.9 us (43%)
  local copies, waits for them, and re-layouts  9.68 us (12%)
  between operations  0.85 us (1%)
    ppermute x5, starting transfers between devices, body(): from_high = lax.ppermute(low, 'space', down)  21.9 us
    pallas_call x4, Pallas kernels, body(): pl.pallas_call(step_kernel, out_shape=published, in_specs=[SMEM] + [VMEM]...  15.1 us
    pallas_call x5, Pallas kernels, body(): pl.pallas_call(gather_local, out_shape=S((128, 6 * elems), BF16), in_spec...  12.8 us
    ppermute x5, starting transfers between devices, body(): top_in = lax.ppermute(top, 'slab', later)  11.3 us
    unnamed x33, local copies, waits for them, and re-layouts  9.68 us
    pallas_call x1, Pallas kernels, body(): pl.pallas_call(prepare, out_shape=[S((1024, 896), BF16), S((512, elems),...  5.12 us
    pallas_call x1, Pallas kernels, body(): pl.pallas_call(last_kernel, out_shape=S((1, 256, elems), F32), in_specs=[...  3.54 us
    ppermute x5, starting transfers between devices, body(): from_low = lax.ppermute(high, 'space', up)  2.62 us
  transfers between devices with their start and end apart: 15, of which 0 were waited for; matrix products, arithmetic and copies ran while one was open for 3% of the time, Pallas kernels for 15%

profile of v1, /device:TPU:0, one launch (start us, length us, event | category | flops | bytes accessed | tf_op | source)
XLA Modules:
  0.0 83.0 jit_solution(5336834658152168307)
XLA Ops:
  0.7 1.6 %copy.10.lift_time = f32[256,64]{1,0:T(8,128)} copy(f32[256,64]{0,1:T(8,128)} %param.13) | data formatting | bytes 131072 | tf_op args[4]
  2.2 5.1 %prepare.1 = (bf16[1024,896]{1,0:T(8,128)(2,1)}, f32[512,256]{1,0:T(8,128)}, bf16[128,1536]{1,0:T(8,128)(2,1)}, f32[64,256]{1,0:T(8,128)}, f32[64,128]{1,0:T(8,128)}, /*index=5*/f32[64,128]{1,0:T(8,128)}) custom-call(s32[1]{0:T(128)S(6)} %copy.13.counts, s32[1]{0:T(128)} %bitcast.first, f32[1,256,256]{2,1,0:T(8,128)} %source.1, f32[64,256]{1,0:T(8,128)} %initial.1, ...), custom_call_target="tpu_custom_call" | custom-call | tf_op jit(solution)/shard_map/prepare/pallas_call | solution.py:189
  7.4 2.4 %collective-permute-start.2 = (f32[64,256]{1,0:T(8,128)}, f32[64,256]{1,0:T(8,128)S(1)}, u32[]{:S(2)}, u32[]{:S(2)}) collective-permute-start(f32[64,256]{1,0:T(8,128)} %get-tuple-element.30), channel_id=1, source_target_pairs={{0,1},{1,2},{2,3},{4,5},{5,6},{6,7},{8,9},{9,10},{10,11},{12,13},{... | collective-permute-start | bytes 196616 | tf_op jit(solution)/shard_map/ppermute | solution.py:200
  9.8 2.4 %collective-permute-start = (f32[64,128]{1,0:T(8,128)}, f32[64,128]{1,0:T(8,128)S(1)}, u32[]{:S(2)}, u32[]{:S(2)}) collective-permute-start(f32[64,128]{1,0:T(8,128)} %get-tuple-element.28), channel_id=1, source_target_pairs={{0,4},{4,8},{8,12},{12,16},{16,20},{20,24},{24,28},{28,0},{1,5},{5... | collective-permute-start | bytes 98312 | tf_op jit(solution)/shard_map/ppermute | solution.py:198
  12.2 3.1 %collective-permute-start.1 = (f32[64,128]{1,0:T(8,128)}, f32[64,128]{1,0:T(8,128)S(1)}, u32[]{:S(2)}, u32[]{:S(2)}) collective-permute-start(f32[64,128]{1,0:T(8,128)} %get-tuple-element.29), channel_id=1, source_target_pairs={{4,0},{8,4},{12,8},{16,12},{20,16},{24,20},{28,24},{0,28},{5,1},{9... | collective-permute-start | bytes 98312 | tf_op jit(solution)/shard_map/ppermute | solution.py:199
  15.3 1.3 %copy.11 = s32[1,1,6,256]{3,1,2,0:T(1,128)} copy(s32[1,1,6,256]{3,2,1,0:T(8,128)} %bitcast.28) | data formatting | bytes 12288
  17.8 2.6 %gather_local.5.local = bf16[128,1536]{1,0:T(8,128)(2,1)} custom-call(bf16[128,1536]{1,0:T(8,128)(2,1)} %get-tuple-element.27.table, s32[1,1536]{1,0:T(1,128)} %bitcast.8), custom_call_target="tpu_custom_call" | custom-call | tf_op jit(solution)/shard_map/gather_local/pallas_call | solution.py:201
  21.1 3.8 %advance.4 = (bf16[128,1536]{1,0:T(8,128)(2,1)}, f32[64,256]{1,0:T(8,128)}, f32[64,128]{1,0:T(8,128)}, f32[64,128]{1,0:T(8,128)}) custom-call(s32[1]{0:T(128)S(6)} %copy.13.counts, bf16[128,1536]{1,0:T(8,128)(2,1)} %gather_local.5.local, f32[64,128]{1,0:T(8,128)} %copy-done.5, f32[64,128]{1,0:T(8,128)} %copy-done.10, f32[64,256]{1,0:T(8,128)} %copy-done, ...), custom_call_target="tpu_custom_call" | custom-call | tf_op jit(solution)/shard_map/advance/pallas_call | solution.py:210
  24.8 3.4 %collective-permute-start.5 = (f32[64,256]{1,0:T(8,128)}, f32[64,256]{1,0:T(8,128)S(1)}, u32[]{:S(2)}, u32[]{:S(2)}) collective-permute-start(f32[64,256]{1,0:T(8,128)} %get-tuple-element.36), channel_id=1, source_target_pairs={{0,1},{1,2},{2,3},{4,5},{5,6},{6,7},{8,9},{9,10},{10,11},{12,13},{... | collective-permute-start | bytes 196616 | tf_op jit(solution)/shard_map/ppermute | solution.py:200
  28.3 4.7 %collective-permute-start.4 = (f32[64,128]{1,0:T(8,128)}, f32[64,128]{1,0:T(8,128)S(1)}, u32[]{:S(2)}, u32[]{:S(2)}) collective-permute-start(f32[64,128]{1,0:T(8,128)} %get-tuple-element.35), channel_id=1, source_target_pairs={{4,0},{8,4},{12,8},{16,12},{20,16},{24,20},{28,24},{0,28},{5,1},{9... | collective-permute-start | bytes 98312 | tf_op jit(solution)/shard_map/ppermute | solution.py:199
  33.0 2.6 %gather_local.6.local = bf16[128,1536]{1,0:T(8,128)(2,1)} custom-call(bf16[128,1536]{1,0:T(8,128)(2,1)} %get-tuple-element.33.table, s32[1,1536]{1,0:T(1,128)} %bitcast.10), custom_call_target="tpu_custom_call" | custom-call | tf_op jit(solution)/shard_map/gather_local/pallas_call | solution.py:201
  36.8 3.8 %advance.5 = (bf16[128,1536]{1,0:T(8,128)(2,1)}, f32[64,256]{1,0:T(8,128)}, f32[64,128]{1,0:T(8,128)}, f32[64,128]{1,0:T(8,128)}) custom-call(s32[1]{0:T(128)S(6)} %copy.13.counts, bf16[128,1536]{1,0:T(8,128)(2,1)} %gather_local.6.local, f32[64,128]{1,0:T(8,128)} %copy-done.7, f32[64,128]{1,0:T(8,128)} %copy-done.12, f32[64,256]{1,0:T(8,128)} %copy-done.1, ...), custom_call_target="tpu_custom_call" | custom-call | tf_op jit(solution)/shard_map/advance/pallas_call | solution.py:210
  40.6 1.7 %collective-permute-start.8 = (f32[64,256]{1,0:T(8,128)}, f32[64,256]{1,0:T(8,128)S(1)}, u32[]{:S(2)}, u32[]{:S(2)}) collective-permute-start(f32[64,256]{1,0:T(8,128)} %get-tuple-element.40), channel_id=1, source_target_pairs={{0,1},{1,2},{2,3},{4,5},{5,6},{6,7},{8,9},{9,10},{10,11},{12,13},{... | collective-permute-start | bytes 196616 | tf_op jit(solution)/shard_map/ppermute | solution.py:200
  42.4 4.7 %collective-permute-start.7 = (f32[64,128]{1,0:T(8,128)}, f32[64,128]{1,0:T(8,128)S(1)}, u32[]{:S(2)}, u32[]{:S(2)}) collective-permute-start(f32[64,128]{1,0:T(8,128)} %get-tuple-element.39), channel_id=1, source_target_pairs={{4,0},{8,4},{12,8},{16,12},{20,16},{24,20},{28,24},{0,28},{5,1},{9... | collective-permute-start | bytes 98312 | tf_op jit(solution)/shard_map/ppermute | solution.py:199
  47.1 2.5 %gather_local.7.local = bf16[128,1536]{1,0:T(8,128)(2,1)} custom-call(bf16[128,1536]{1,0:T(8,128)(2,1)} %get-tuple-element.37.table, s32[1,1536]{1,0:T(1,128)} %bitcast.12), custom_call_target="tpu_custom_call" | custom-call | tf_op jit(solution)/shard_map/gather_local/pallas_call | solution.py:201
  50.9 3.8 %advance.6 = (bf16[128,1536]{1,0:T(8,128)(2,1)}, f32[64,256]{1,0:T(8,128)}, f32[64,128]{1,0:T(8,128)}, f32[64,128]{1,0:T(8,128)}) custom-call(s32[1]{0:T(128)S(6)} %copy.13.counts, bf16[128,1536]{1,0:T(8,128)(2,1)} %gather_local.7.local, f32[64,128]{1,0:T(8,128)} %copy-done.8, f32[64,128]{1,0:T(8,128)} %copy-done.13, f32[64,256]{1,0:T(8,128)} %copy-done.2, ...), custom_call_target="tpu_custom_call" | custom-call | tf_op jit(solution)/shard_map/advance/pallas_call | solution.py:210
  54.7 1.9 %collective-permute-start.11 = (f32[64,256]{1,0:T(8,128)}, f32[64,256]{1,0:T(8,128)S(1)}, u32[]{:S(2)}, u32[]{:S(2)}) collective-permute-start(f32[64,256]{1,0:T(8,128)} %get-tuple-element.44), channel_id=1, source_target_pairs={{0,1},{1,2},{2,3},{4,5},{5,6},{6,7},{8,9},{9,10},{10,11},{12,13},{... | collective-permute-start | bytes 196616 | tf_op jit(solution)/shard_map/ppermute | solution.py:200
  56.7 4.7 %collective-permute-start.10 = (f32[64,128]{1,0:T(8,128)}, f32[64,128]{1,0:T(8,128)S(1)}, u32[]{:S(2)}, u32[]{:S(2)}) collective-permute-start(f32[64,128]{1,0:T(8,128)} %get-tuple-element.43), channel_id=1, source_target_pairs={{4,0},{8,4},{12,8},{16,12},{20,16},{24,20},{28,24},{0,28},{5,1},{9... | collective-permute-start | bytes 98312 | tf_op jit(solution)/shard_map/ppermute | solution.py:199
  61.4 2.5 %gather_local.8.local = bf16[128,1536]{1,0:T(8,128)(2,1)} custom-call(bf16[128,1536]{1,0:T(8,128)(2,1)} %get-tuple-element.41.table, s32[1,1536]{1,0:T(1,128)} %bitcast.14), custom_call_target="tpu_custom_call" | custom-call | tf_op jit(solution)/shard_map/gather_local/pallas_call | solution.py:201
  65.2 3.8 %advance.7 = (bf16[128,1536]{1,0:T(8,128)(2,1)}, f32[64,256]{1,0:T(8,128)}, f32[64,128]{1,0:T(8,128)}, f32[64,128]{1,0:T(8,128)}) custom-call(s32[1]{0:T(128)S(6)} %copy.13.counts, bf16[128,1536]{1,0:T(8,128)(2,1)} %gather_local.8.local, f32[64,128]{1,0:T(8,128)} %copy-done.9, f32[64,128]{1,0:T(8,128)} %copy-done.14, f32[64,256]{1,0:T(8,128)} %copy-done.3, ...), custom_call_target="tpu_custom_call" | custom-call | tf_op jit(solution)/shard_map/advance/pallas_call | solution.py:210
  69.0 1.9 %collective-permute-start.14 = (f32[64,256]{1,0:T(8,128)}, f32[64,256]{1,0:T(8,128)S(1)}, u32[]{:S(2)}, u32[]{:S(2)}) collective-permute-start(f32[64,256]{1,0:T(8,128)} %get-tuple-element.48), channel_id=1, source_target_pairs={{0,1},{1,2},{2,3},{4,5},{5,6},{6,7},{8,9},{9,10},{10,11},{12,13},{... | collective-permute-start | bytes 196616 | tf_op jit(solution)/shard_map/ppermute | solution.py:200
  71.0 4.7 %collective-permute-start.13 = (f32[64,128]{1,0:T(8,128)}, f32[64,128]{1,0:T(8,128)S(1)}, u32[]{:S(2)}, u32[]{:S(2)}) collective-permute-start(f32[64,128]{1,0:T(8,128)} %get-tuple-element.47), channel_id=1, source_target_pairs={{4,0},{8,4},{12,8},{16,12},{20,16},{24,20},{28,24},{0,28},{5,1},{9... | collective-permute-start | bytes 98312 | tf_op jit(solution)/shard_map/ppermute | solution.py:199
  75.7 2.6 %gather_local.9.local = bf16[128,1536]{1,0:T(8,128)(2,1)} custom-call(bf16[128,1536]{1,0:T(8,128)(2,1)} %get-tuple-element.45.table, s32[1,1536]{1,0:T(1,128)} %bitcast.16), custom_call_target="tpu_custom_call" | custom-call | tf_op jit(solution)/shard_map/gather_local/pallas_call | solution.py:201
  79.5 3.5 %advance_last.1 = f32[1,256,256]{2,1,0:T(8,128)} custom-call(s32[1]{0:T(128)S(6)} %copy.13.counts, bf16[128,1536]{1,0:T(8,128)(2,1)} %gather_local.9.local, f32[64,128]{1,0:T(8,128)} %copy-done.6, f32[64,128]{1,0:T(8,128)} %copy-done.11, f32[64,256]{1,0:T(8,128)} %copy-done.4, bf16[1024,896]{1,0:T(8,128)(2,1)} %get-tuple-element.31.weight, ...), custom_call_target="tpu_custom_call" | custom-call | tf_op jit(solution)/shard_map/advance_last/pallas_call | solution.py:219
  (50 shorter events, 7.1 us)
Async XLA Ops:
  7.4 13.0 %collective-permute-start.2 = (f32[64,256]{1,0:T(8,128)}, f32[64,256]{1,0:T(8,128)S(1)}, u32[]{:S(2)}, u32[]{:S(2)}) collective-permute-start(f32[64,256]{1,0:T(8,128)} %get-tuple-element.30), channel_id=1, source_target_pairs={{0,1},{1,2},{2,3},{4,5},{5,6},{6,7},{8,9},{9,10},{10,11},{12,13},{... | collective-permute-start | bytes 196616 | tf_op jit(solution)/shard_map/ppermute | solution.py:200
  9.8 10.6 %collective-permute-start = (f32[64,128]{1,0:T(8,128)}, f32[64,128]{1,0:T(8,128)S(1)}, u32[]{:S(2)}, u32[]{:S(2)}) collective-permute-start(f32[64,128]{1,0:T(8,128)} %get-tuple-element.28), channel_id=1, source_target_pairs={{0,4},{4,8},{8,12},{12,16},{16,20},{20,24},{24,28},{28,0},{1,5},{5... | collective-permute-start | bytes 98312 | tf_op jit(solution)/shard_map/ppermute | solution.py:198
  12.2 8.2 %collective-permute-start.1 = (f32[64,128]{1,0:T(8,128)}, f32[64,128]{1,0:T(8,128)S(1)}, u32[]{:S(2)}, u32[]{:S(2)}) collective-permute-start(f32[64,128]{1,0:T(8,128)} %get-tuple-element.29), channel_id=1, source_target_pairs={{4,0},{8,4},{12,8},{16,12},{20,16},{24,20},{28,24},{0,28},{5,1},{9... | collective-permute-start | bytes 98312 | tf_op jit(solution)/shard_map/ppermute | solution.py:199
  20.4 0.6 copy-start.5
  20.4 0.6 copy-start
  24.8 10.7 %collective-permute-start.5 = (f32[64,256]{1,0:T(8,128)}, f32[64,256]{1,0:T(8,128)S(1)}, u32[]{:S(2)}, u32[]{:S(2)}) collective-permute-start(f32[64,256]{1,0:T(8,128)} %get-tuple-element.36), channel_id=1, source_target_pairs={{0,1},{1,2},{2,3},{4,5},{5,6},{6,7},{8,9},{9,10},{10,11},{12,13},{... | collective-permute-start | bytes 196616 | tf_op jit(solution)/shard_map/ppermute | solution.py:200
  28.2 7.3 %collective-permute-start.3 = (f32[64,128]{1,0:T(8,128)}, f32[64,128]{1,0:T(8,128)S(1)}, u32[]{:S(2)}, u32[]{:S(2)}) collective-permute-start(f32[64,128]{1,0:T(8,128)} %get-tuple-element.34), channel_id=1, source_target_pairs={{0,4},{4,8},{8,12},{12,16},{16,20},{20,24},{24,28},{28,0},{1,5},{5... | collective-permute-start | bytes 98312 | tf_op jit(solution)/shard_map/ppermute | solution.py:198
  28.3 7.3 %collective-permute-start.4 = (f32[64,128]{1,0:T(8,128)}, f32[64,128]{1,0:T(8,128)S(1)}, u32[]{:S(2)}, u32[]{:S(2)}) collective-permute-start(f32[64,128]{1,0:T(8,128)} %get-tuple-element.35), channel_id=1, source_target_pairs={{4,0},{8,4},{12,8},{16,12},{20,16},{24,20},{28,24},{0,28},{5,1},{9... | collective-permute-start | bytes 98312 | tf_op jit(solution)/shard_map/ppermute | solution.py:199
  35.6 0.6 copy-start.7
  36.2 0.6 copy-start.1
  40.6 9.1 %collective-permute-start.8 = (f32[64,256]{1,0:T(8,128)}, f32[64,256]{1,0:T(8,128)S(1)}, u32[]{:S(2)}, u32[]{:S(2)}) collective-permute-start(f32[64,256]{1,0:T(8,128)} %get-tuple-element.40), channel_id=1, source_target_pairs={{0,1},{1,2},{2,3},{4,5},{5,6},{6,7},{8,9},{9,10},{10,11},{12,13},{... | collective-permute-start | bytes 196616 | tf_op jit(solution)/shard_map/ppermute | solution.py:200
  42.3 7.3 %collective-permute-start.6 = (f32[64,128]{1,0:T(8,128)}, f32[64,128]{1,0:T(8,128)S(1)}, u32[]{:S(2)}, u32[]{:S(2)}) collective-permute-start(f32[64,128]{1,0:T(8,128)} %get-tuple-element.38), channel_id=1, source_target_pairs={{0,4},{4,8},{8,12},{12,16},{16,20},{20,24},{24,28},{28,0},{1,5},{5... | collective-permute-start | bytes 98312 | tf_op jit(solution)/shard_map/ppermute | solution.py:198
  42.4 7.3 %collective-permute-start.7 = (f32[64,128]{1,0:T(8,128)}, f32[64,128]{1,0:T(8,128)S(1)}, u32[]{:S(2)}, u32[]{:S(2)}) collective-permute-start(f32[64,128]{1,0:T(8,128)} %get-tuple-element.39), channel_id=1, source_target_pairs={{4,0},{8,4},{12,8},{16,12},{20,16},{24,20},{28,24},{0,28},{5,1},{9... | collective-permute-start | bytes 98312 | tf_op jit(solution)/shard_map/ppermute | solution.py:199
  49.7 0.6 copy-start.8
  50.3 0.6 copy-start.2
  54.7 9.3 %collective-permute-start.11 = (f32[64,256]{1,0:T(8,128)}, f32[64,256]{1,0:T(8,128)S(1)}, u32[]{:S(2)}, u32[]{:S(2)}) collective-permute-start(f32[64,256]{1,0:T(8,128)} %get-tuple-element.44), channel_id=1, source_target_pairs={{0,1},{1,2},{2,3},{4,5},{5,6},{6,7},{8,9},{9,10},{10,11},{12,13},{... | collective-permute-start | bytes 196616 | tf_op jit(solution)/shard_map/ppermute | solution.py:200
  56.6 7.3 %collective-permute-start.9 = (f32[64,128]{1,0:T(8,128)}, f32[64,128]{1,0:T(8,128)S(1)}, u32[]{:S(2)}, u32[]{:S(2)}) collective-permute-start(f32[64,128]{1,0:T(8,128)} %get-tuple-element.42), channel_id=1, source_target_pairs={{0,4},{4,8},{8,12},{12,16},{16,20},{20,24},{24,28},{28,0},{1,5},{5... | collective-permute-start | bytes 98312 | tf_op jit(solution)/shard_map/ppermute | solution.py:198
  56.7 7.3 %collective-permute-start.10 = (f32[64,128]{1,0:T(8,128)}, f32[64,128]{1,0:T(8,128)S(1)}, u32[]{:S(2)}, u32[]{:S(2)}) collective-permute-start(f32[64,128]{1,0:T(8,128)} %get-tuple-element.43), channel_id=1, source_target_pairs={{4,0},{8,4},{12,8},{16,12},{20,16},{24,20},{28,24},{0,28},{5,1},{9... | collective-permute-start | bytes 98312 | tf_op jit(solution)/shard_map/ppermute | solution.py:199
  63.9 0.6 copy-start.9
  64.6 0.6 copy-start.3
  69.0 9.3 %collective-permute-start.14 = (f32[64,256]{1,0:T(8,128)}, f32[64,256]{1,0:T(8,128)S(1)}, u32[]{:S(2)}, u32[]{:S(2)}) collective-permute-start(f32[64,256]{1,0:T(8,128)} %get-tuple-element.48), channel_id=1, source_target_pairs={{0,1},{1,2},{2,3},{4,5},{5,6},{6,7},{8,9},{9,10},{10,11},{12,13},{... | collective-permute-start | bytes 196616 | tf_op jit(solution)/shard_map/ppermute | solution.py:200
  70.9 7.3 %collective-permute-start.12 = (f32[64,128]{1,0:T(8,128)}, f32[64,128]{1,0:T(8,128)S(1)}, u32[]{:S(2)}, u32[]{:S(2)}) collective-permute-start(f32[64,128]{1,0:T(8,128)} %get-tuple-element.46), channel_id=1, source_target_pairs={{0,4},{4,8},{8,12},{12,16},{16,20},{20,24},{24,28},{28,0},{1,5},{5... | collective-permute-start | bytes 98312 | tf_op jit(solution)/shard_map/ppermute | solution.py:198
  71.0 7.3 %collective-permute-start.13 = (f32[64,128]{1,0:T(8,128)}, f32[64,128]{1,0:T(8,128)S(1)}, u32[]{:S(2)}, u32[]{:S(2)}) collective-permute-start(f32[64,128]{1,0:T(8,128)} %get-tuple-element.47), channel_id=1, source_target_pairs={{4,0},{8,4},{12,8},{16,12},{20,16},{24,20},{28,24},{0,28},{5,1},{9... | collective-permute-start | bytes 98312 | tf_op jit(solution)/shard_map/ppermute | solution.py:199
  78.8 0.6 copy-start.4
  (6 other events, 3.7 us)

commit v2 on v1

--- a/solution.py
+++ b/solution.py
@@ -87,7 +87,7 @@
         return mm(inv_hi, x_hi) + (mm(inv_hi, x_lo) + mm(inv_lo, x_hi))
 
     start = initial[...] * jnp.where(first[0] > 0, 1.0, 0.0)
-    lt_hi, lt_lo = split(lift_time[...])
+    lt_hi, lt_lo = split(lift_time[...].T)
     st_hi, st_lo = split(start)
     rhs = source[0] + (mm(lt_hi, st_hi) + (mm(lt_hi, st_lo) + mm(lt_lo, st_hi)))
     rows = solve(*split(rhs)) * live_of(counts, elems)
@@ -109,10 +109,10 @@
 
 
 def gather_local(table, links, out):
-    elems = links.shape[1] // 6
+    elems = links.shape[1]
     for face in range(6):
         cols = slice(face * elems, (face + 1) * elems)
-        pick = one_hot(iota((6 * elems, elems), 0) == links[:, cols])
+        pick = one_hot(iota((6 * elems, elems), 0) == links[face : face + 1, :])
         out[:, cols] = mm(table[...], pick).astype(BF16)
 
 
@@ -131,9 +131,9 @@
     imported = jnp.concatenate(sides, axis=1)
     for face in range(6):
         cols = slice(face * elems, (face + 1) * elems)
-        pick = one_hot(iota((2 * peer, elems), 0) + 6 * elems == links[:, cols])
+        pick = one_hot(iota((2 * peer, elems), 0) + 6 * elems == links[face : face + 1, :])
         got = local[:, cols].astype(F32) + mm(imported, pick)
-        turn = jnp.broadcast_to(orient[:, cols], (8, elems))
+        turn = jnp.broadcast_to(orient[face : face + 1, :], (8, elems))
         swap = (turn & 4) > 0
         rev_a = (turn & 1) > 0
         rev_b = (turn & 2) > 0
@@ -168,15 +168,14 @@
 def body(source, initial, inverse, lift, lift_time, links, orient, exports, counts):
     elems = links.shape[1]
     peer = exports.shape[0] // 2
-    links = links.reshape(1, 6 * elems)
-    orient = orient.reshape(1, 6 * elems)
     exports = exports.reshape(1, 2 * peer)
     first = (lax.axis_index("slab") == 0).astype(jnp.int32).reshape(1)
     spaces = lax.axis_size("space")
     up = [(i, (i + 1) % spaces) for i in range(spaces)]
     down = [(b, a) for a, b in up]
     later = [(i, i + 1) for i in range(lax.axis_size("slab") - 1)]
-    S = jax.ShapeDtypeStruct
+    S = pltpu.VMEM
+    params = pltpu.CompilerParams(vmem_limit_bytes=24 * 1024 * 1024)
     published = [
         S((128, 6 * elems), BF16),
         S((64, elems), F32),
@@ -192,8 +191,9 @@
         in_specs=[SMEM, SMEM] + [VMEM] * 6,
         out_specs=[VMEM] * 6,
         scratch_shapes=[rows_scratch],
+        compiler_params=params,
         name="prepare",
-    )(counts, first, source, initial, inverse, lift, lift_time, exports)
+    )(counts, first, source, initial, inverse, lift, lift_time.T, exports)
     for step in range(1, ITERS):
         from_low = lax.ppermute(high, "space", up)
         from_high = lax.ppermute(low, "space", down)
@@ -203,8 +203,12 @@
             out_shape=S((128, 6 * elems), BF16),
             in_specs=[VMEM] * 2,
             out_specs=VMEM,
+            compiler_params=params,
             name="gather_local",
         )(table, links)
+        from_low, from_high, top_in = (
+            pltpu.with_memory_space_constraint(x, pltpu.VMEM) for x in (from_low, from_high, top_in)
+        )
         args = (counts, local, from_low, from_high, top_in, weight, base, links, orient)
         if step < ITERS - 1:
             table, top, low, high = pl.pallas_call(
@@ -213,15 +217,17 @@
                 in_specs=[SMEM] + [VMEM] * 9,
                 out_specs=[VMEM] * 4,
                 scratch_shapes=[nbr_scratch, rows_scratch],
+                compiler_params=params,
                 name="advance",
             )(*args, exports)
         else:
             out = pl.pallas_call(
                 last_kernel,
-                out_shape=S((1, 256, elems), F32),
+                out_shape=jax.ShapeDtypeStruct((1, 256, elems), F32),
                 in_specs=[SMEM] + [VMEM] * 8,
                 out_specs=VMEM,
                 scratch_shapes=[nbr_scratch, rows_scratch],
+                compiler_params=params,
                 name="advance_last",
             )(*args)
     return out

time: 83.6 us -> 61.9 us (0.74)
  Pallas kernels: 36.5 us -> 13.5 us
  waiting for transfers between devices: 0.04 us -> 5.4 us
  local copies, waits for them, and re-layouts: 9.68 us -> 5.95 us
    pallas_call x4, Pallas kernels: 15.1 us -> 5.18 us  [body(): pl.pallas_call(step_kernel, out_shape=published, in_specs=[SMEM] + [VMEM]...]
    pallas_call x5, Pallas kernels: 12.8 us -> 3.96 us  [body(): pl.pallas_call(gather_local, out_shape=S((128, 6 * elems), BF16), in_spec...]
    ppermute x5, waiting for transfers between devices: 0.01 us -> 5.38 us  [body(): from_low = lax.ppermute(high, 'space', up)]
    unnamed x33 -> x18, local copies, waits for them, and re-layouts: 9.68 us -> 5.95 us
    pallas_call x1, Pallas kernels: 5.12 us -> 2.64 us  [body(): pl.pallas_call(prepare, out_shape=[S((1024, 896), BF16), S((512, elems),...]
    pallas_call x1, Pallas kernels: 3.54 us -> 1.68 us  [body(): pl.pallas_call(last_kernel, out_shape=jax.ShapeDtypeStruct((1, 256, elems...]
  transfers between devices with their start and end apart: 15 -> 15, of which waited for: 0 -> 5; matrix products, arithmetic and copies ran while one was open for 3% -> 0% of each run, Pallas kernels for 15% -> 6%
where the time goes in v2:
time: 61.9 us; the launch traced here: 61.4 us
  starting transfers between devices  35.8 us (58%)
  Pallas kernels  13.5 us (22%)
  local copies, waits for them, and re-layouts  5.95 us (10%)
  waiting for transfers between devices  5.4 us (9%)
  between operations  0.84 us (1%)
    ppermute x5, starting transfers between devices, body(): from_high = lax.ppermute(low, 'space', down)  21.4 us
    ppermute x5, starting transfers between devices, body(): top_in = lax.ppermute(top, 'slab', later)  11.2 us
    unnamed x18, local copies, waits for them, and re-layouts  5.95 us
    ppermute x5, waiting for transfers between devices, body(): from_low = lax.ppermute(high, 'space', up)  5.38 us
    pallas_call x4, Pallas kernels, body(): pl.pallas_call(step_kernel, out_shape=published, in_specs=[SMEM] + [VMEM]...  5.18 us
    pallas_call x5, Pallas kernels, body(): pl.pallas_call(gather_local, out_shape=S((128, 6 * elems), BF16), in_spec...  3.96 us
    ppermute x5, starting transfers between devices, body(): from_low = lax.ppermute(high, 'space', up)  3.16 us
    pallas_call x1, Pallas kernels, body(): pl.pallas_call(prepare, out_shape=[S((1024, 896), BF16), S((512, elems),...  2.64 us
  transfers between devices with their start and end apart: 15, of which 5 were waited for; matrix products, arithmetic and copies ran while one was open for 0% of the time, Pallas kernels for 6%

profile of v2, /device:TPU:0, one launch (start us, length us, event | category | flops | bytes accessed | tf_op | source)
XLA Modules:
  0.0 61.4 jit_solution(425405368151135020)
XLA Ops:
  0.7 1.0 %copy-done.2 = f32[256,384]{1,0:T(8,128)S(1)} copy-done((f32[256,384]{1,0:T(8,128)S(1)}, f32[256,384]{1,0:T(8,128)}, u32[]{:S(2)}) %copy-start.2) | copy-done | bytes 393240
  1.7 0.9 %copy-done.3 = f32[1,256,256]{2,1,0:T(8,128)S(1)} copy-done((f32[1,256,256]{2,1,0:T(8,128)S(1)}, f32[1,256,256]{2,1,0:T(8,128)}, u32[]{:S(2)}) %copy-start.3) | copy-done | bytes 262168
  2.6 0.9 %copy-done.4 = f32[256,256]{1,0:T(8,128)S(1)} copy-done((f32[256,256]{1,0:T(8,128)S(1)}, f32[256,256]{1,0:T(8,128)}, u32[]{:S(2)}) %copy-start.4) | copy-done | bytes 262168
  5.9 2.6 %prepare.1 = (bf16[1024,896]{1,0:T(8,128)(2,1)S(1)}, f32[512,256]{1,0:T(8,128)S(1)}, bf16[128,1536]{1,0:T(8,128)(2,1)S(1)}, f32[64,256]{1,0:T(8,128)S(1)}, f32[64,128]{1,0:T(8,128)S(1)}, /*index=5*/f32[64,128]{1,0:T(8,128)S(1)}) custom-call(s32[1]{0:T(128)S(6)} %copy.10.counts, s32[1]{0:T(128)} %bitcast.first, f32[1,256,256]{2,1,0:T(8,128)S(1)} %copy-done.3, ...), custom_call_target="tpu_custom_call" | custom-call | tf_op jit(solution)/shard_map/prepare/pallas_call | solution.py:188
  8.6 2.4 %collective-permute-start.2 = (f32[64,256]{1,0:T(8,128)S(1)}, f32[64,256]{1,0:T(8,128)S(1)}, u32[]{:S(2)}, u32[]{:S(2)}) collective-permute-start(f32[64,256]{1,0:T(8,128)S(1)} %get-tuple-element.30), channel_id=1, source_target_pairs={{0,1},{1,2},{2,3},{4,5},{5,6},{6,7},{8,9},{9,10},{10,11},{12,13},{... | collective-permute-start | bytes 196616 | tf_op jit(solution)/shard_map/ppermute | solution.py:200
  11.0 2.4 %collective-permute-start = (f32[64,128]{1,0:T(8,128)S(1)}, f32[64,128]{1,0:T(8,128)S(1)}, u32[]{:S(2)}, u32[]{:S(2)}) collective-permute-start(f32[64,128]{1,0:T(8,128)S(1)} %get-tuple-element.28), channel_id=1, source_target_pairs={{0,4},{4,8},{8,12},{12,16},{16,20},{20,24},{24,28},{28,0},{1,5},{5... | collective-permute-start | bytes 98312 | tf_op jit(solution)/shard_map/ppermute | solution.py:198
  13.4 3.1 %collective-permute-start.1 = (f32[64,128]{1,0:T(8,128)S(1)}, f32[64,128]{1,0:T(8,128)S(1)}, u32[]{:S(2)}, u32[]{:S(2)}) collective-permute-start(f32[64,128]{1,0:T(8,128)S(1)} %get-tuple-element.29), channel_id=1, source_target_pairs={{4,0},{8,4},{12,8},{16,12},{20,16},{24,20},{28,24},{0,28},{5,1},{9... | collective-permute-start | bytes 98312 | tf_op jit(solution)/shard_map/ppermute | solution.py:199
  18.3 1.3 %advance.4 = (bf16[128,1536]{1,0:T(8,128)(2,1)S(1)}, f32[64,256]{1,0:T(8,128)S(1)}, f32[64,128]{1,0:T(8,128)S(1)}, f32[64,128]{1,0:T(8,128)S(1)}) custom-call(s32[1]{0:T(128)S(6)} %copy.10.counts, bf16[128,1536]{1,0:T(8,128)(2,1)S(1)} %gather_local.5.local, f32[64,128]{1,0:T(8,128)S(1)} %collective-permute-done.from_low, ...), custom_call_target="tpu_custom_call" | custom-call | tf_op jit(solution)/shard_map/advance/pallas_call | solution.py:214
  19.6 3.1 %collective-permute-start.5 = (f32[64,256]{1,0:T(8,128)S(1)}, f32[64,256]{1,0:T(8,128)S(1)}, u32[]{:S(2)}, u32[]{:S(2)}) collective-permute-start(f32[64,256]{1,0:T(8,128)S(1)} %get-tuple-element.36), channel_id=1, source_target_pairs={{0,1},{1,2},{2,3},{4,5},{5,6},{6,7},{8,9},{9,10},{10,11},{12,13},{... | collective-permute-start | bytes 196616 | tf_op jit(solution)/shard_map/ppermute | solution.py:200
  23.3 4.2 %collective-permute-start.4 = (f32[64,128]{1,0:T(8,128)S(1)}, f32[64,128]{1,0:T(8,128)S(1)}, u32[]{:S(2)}, u32[]{:S(2)}) collective-permute-start(f32[64,128]{1,0:T(8,128)S(1)} %get-tuple-element.35), channel_id=1, source_target_pairs={{4,0},{8,4},{12,8},{16,12},{20,16},{24,20},{28,24},{0,28},{5,1},{9... | collective-permute-start | bytes 98312 | tf_op jit(solution)/shard_map/ppermute | solution.py:199
  28.3 1.4 %collective-permute-done.3.from_low = f32[64,128]{1,0:T(8,128)S(1)} collective-permute-done((f32[64,128]{1,0:T(8,128)S(1)}, f32[64,128]{1,0:T(8,128)S(1)}, u32[]{:S(2)}, u32[]{:S(2)}) %collective-permute-start.3) | collective-permute-done | bytes 32800 | tf_op jit(solution)/shard_map/ppermute | solution.py:198
  29.7 1.3 %advance.5 = (bf16[128,1536]{1,0:T(8,128)(2,1)S(1)}, f32[64,256]{1,0:T(8,128)S(1)}, f32[64,128]{1,0:T(8,128)S(1)}, f32[64,128]{1,0:T(8,128)S(1)}) custom-call(s32[1]{0:T(128)S(6)} %copy.10.counts, bf16[128,1536]{1,0:T(8,128)(2,1)S(1)} %gather_local.6.local, f32[64,128]{1,0:T(8,128)S(1)} %collective-permute-done.3.from_low, ...), custom_call_target="tpu_custom_call" | custom-call | tf_op jit(solution)/shard_map/advance/pallas_call | solution.py:214
  31.0 2.0 %collective-permute-start.8 = (f32[64,256]{1,0:T(8,128)S(1)}, f32[64,256]{1,0:T(8,128)S(1)}, u32[]{:S(2)}, u32[]{:S(2)}) collective-permute-start(f32[64,256]{1,0:T(8,128)S(1)} %get-tuple-element.40), channel_id=1, source_target_pairs={{0,1},{1,2},{2,3},{4,5},{5,6},{6,7},{8,9},{9,10},{10,11},{12,13},{... | collective-permute-start | bytes 196616 | tf_op jit(solution)/shard_map/ppermute | solution.py:200
  33.1 4.7 %collective-permute-start.7 = (f32[64,128]{1,0:T(8,128)S(1)}, f32[64,128]{1,0:T(8,128)S(1)}, u32[]{:S(2)}, u32[]{:S(2)}) collective-permute-start(f32[64,128]{1,0:T(8,128)S(1)} %get-tuple-element.39), channel_id=1, source_target_pairs={{4,0},{8,4},{12,8},{16,12},{20,16},{24,20},{28,24},{0,28},{5,1},{9... | collective-permute-start | bytes 98312 | tf_op jit(solution)/shard_map/ppermute | solution.py:199
  38.6 1.2 %collective-permute-done.6.from_low = f32[64,128]{1,0:T(8,128)S(1)} collective-permute-done((f32[64,128]{1,0:T(8,128)S(1)}, f32[64,128]{1,0:T(8,128)S(1)}, u32[]{:S(2)}, u32[]{:S(2)}) %collective-permute-start.6) | collective-permute-done | bytes 32800 | tf_op jit(solution)/shard_map/ppermute | solution.py:198
  39.8 1.3 %advance.6 = (bf16[128,1536]{1,0:T(8,128)(2,1)S(1)}, f32[64,256]{1,0:T(8,128)S(1)}, f32[64,128]{1,0:T(8,128)S(1)}, f32[64,128]{1,0:T(8,128)S(1)}) custom-call(s32[1]{0:T(128)S(6)} %copy.10.counts, bf16[128,1536]{1,0:T(8,128)(2,1)S(1)} %gather_local.7.local, f32[64,128]{1,0:T(8,128)S(1)} %collective-permute-done.6.from_low, ...), custom_call_target="tpu_custom_call" | custom-call | tf_op jit(solution)/shard_map/advance/pallas_call | solution.py:214
  41.1 1.8 %collective-permute-start.11 = (f32[64,256]{1,0:T(8,128)S(1)}, f32[64,256]{1,0:T(8,128)S(1)}, u32[]{:S(2)}, u32[]{:S(2)}) collective-permute-start(f32[64,256]{1,0:T(8,128)S(1)} %get-tuple-element.44), channel_id=1, source_target_pairs={{0,1},{1,2},{2,3},{4,5},{5,6},{6,7},{8,9},{9,10},{10,11},{12,13},{... | collective-permute-start | bytes 196616 | tf_op jit(solution)/shard_map/ppermute | solution.py:200
  42.9 4.7 %collective-permute-start.10 = (f32[64,128]{1,0:T(8,128)S(1)}, f32[64,128]{1,0:T(8,128)S(1)}, u32[]{:S(2)}, u32[]{:S(2)}) collective-permute-start(f32[64,128]{1,0:T(8,128)S(1)} %get-tuple-element.43), channel_id=1, source_target_pairs={{4,0},{8,4},{12,8},{16,12},{20,16},{24,20},{28,24},{0,28},{5,1},{9... | collective-permute-start | bytes 98312 | tf_op jit(solution)/shard_map/ppermute | solution.py:199
  48.4 1.3 %collective-permute-done.9.from_low = f32[64,128]{1,0:T(8,128)S(1)} collective-permute-done((f32[64,128]{1,0:T(8,128)S(1)}, f32[64,128]{1,0:T(8,128)S(1)}, u32[]{:S(2)}, u32[]{:S(2)}) %collective-permute-start.9) | collective-permute-done | bytes 32800 | tf_op jit(solution)/shard_map/ppermute | solution.py:198
  49.7 1.3 %advance.7 = (bf16[128,1536]{1,0:T(8,128)(2,1)S(1)}, f32[64,256]{1,0:T(8,128)S(1)}, f32[64,128]{1,0:T(8,128)S(1)}, f32[64,128]{1,0:T(8,128)S(1)}) custom-call(s32[1]{0:T(128)S(6)} %copy.10.counts, bf16[128,1536]{1,0:T(8,128)(2,1)S(1)} %gather_local.8.local, f32[64,128]{1,0:T(8,128)S(1)} %collective-permute-done.9.from_low, ...), custom_call_target="tpu_custom_call" | custom-call | tf_op jit(solution)/shard_map/advance/pallas_call | solution.py:214
  51.1 1.9 %collective-permute-start.14 = (f32[64,256]{1,0:T(8,128)S(1)}, f32[64,256]{1,0:T(8,128)S(1)}, u32[]{:S(2)}, u32[]{:S(2)}) collective-permute-start(f32[64,256]{1,0:T(8,128)S(1)} %get-tuple-element.48), channel_id=1, source_target_pairs={{0,1},{1,2},{2,3},{4,5},{5,6},{6,7},{8,9},{9,10},{10,11},{12,13},{... | collective-permute-start | bytes 196616 | tf_op jit(solution)/shard_map/ppermute | solution.py:200
  53.1 4.7 %collective-permute-start.13 = (f32[64,128]{1,0:T(8,128)S(1)}, f32[64,128]{1,0:T(8,128)S(1)}, u32[]{:S(2)}, u32[]{:S(2)}) collective-permute-start(f32[64,128]{1,0:T(8,128)S(1)} %get-tuple-element.47), channel_id=1, source_target_pairs={{4,0},{8,4},{12,8},{16,12},{20,16},{24,20},{28,24},{0,28},{5,1},{9... | collective-permute-start | bytes 98312 | tf_op jit(solution)/shard_map/ppermute | solution.py:199
  58.6 1.2 %collective-permute-done.12.from_low = f32[64,128]{1,0:T(8,128)S(1)} collective-permute-done((f32[64,128]{1,0:T(8,128)S(1)}, f32[64,128]{1,0:T(8,128)S(1)}, u32[]{:S(2)}, u32[]{:S(2)}) %collective-permute-start.12) | collective-permute-done | bytes 32800 | tf_op jit(solution)/shard_map/ppermute | solution.py:198
  59.7 1.7 %advance_last.1 = f32[1,256,256]{2,1,0:T(8,128)} custom-call(s32[1]{0:T(128)S(6)} %copy.10.counts, bf16[128,1536]{1,0:T(8,128)(2,1)S(1)} %gather_local.9.local, f32[64,128]{1,0:T(8,128)S(1)} %collective-permute-done.12.from_low, f32[64,128]{1,0:T(8,128)S(1)} %collective-permute-done.13.from_high, f32[64,256]{1,0:T(8,128)S(1)} %collective-permute-done.14.top_in, ...), custom_call_target="tpu_custom_call" | custom-call | tf_op jit(solution)/shard_map/advance_last/pallas_call | solution.py:224
  (35 shorter events, 8.1 us)
Async XLA Ops:
  0.0 18.3 %copy-start.5 = (s32[6,256]{1,0:T(8,128)S(1)}, s32[6,256]{1,0:T(8,128)}, u32[]{:S(2)}) copy-start(s32[6,256]{1,0:T(8,128)} %orient.9) | copy-start | bytes 18436
  0.7 1.0 %copy-start.2 = (f32[256,384]{1,0:T(8,128)S(1)}, f32[256,384]{1,0:T(8,128)}, u32[]{:S(2)}) copy-start(f32[256,384]{1,0:T(8,128)} %lift.1) | copy-start | bytes 1179652
  1.7 0.9 %copy-start.3 = (f32[1,256,256]{2,1,0:T(8,128)S(1)}, f32[1,256,256]{2,1,0:T(8,128)}, u32[]{:S(2)}) copy-start(f32[1,256,256]{2,1,0:T(8,128)} %source.1) | copy-start | bytes 786436
  2.6 0.9 %copy-start.4 = (f32[256,256]{1,0:T(8,128)S(1)}, f32[256,256]{1,0:T(8,128)}, u32[]{:S(2)}) copy-start(f32[256,256]{1,0:T(8,128)} %inverse.1) | copy-start | bytes 786436
  3.6 0.8 %copy-start.6 = (f32[64,256]{1,0:T(8,128)S(1)}, f32[64,256]{1,0:T(8,128)}, u32[]{:S(2)}) copy-start(f32[64,256]{1,0:T(8,128)} %initial.1) | copy-start | bytes 196612
  4.4 0.8 %copy-start.7 = (f32[256,64]{0,1:T(8,128)S(1)}, f32[256,64]{0,1:T(8,128)}, u32[]{:S(2)}) copy-start(f32[256,64]{0,1:T(8,128)} %param.13) | copy-start | bytes 196612
  5.2 0.7 %copy-start.8 = (s32[256]{0:T(256)S(1)}, s32[256]{0:T(256)}, u32[]{:S(2)}) copy-start(s32[256]{0:T(256)} %param.16) | copy-start | bytes 3076
  8.6 9.7 %collective-permute-start.2 = (f32[64,256]{1,0:T(8,128)S(1)}, f32[64,256]{1,0:T(8,128)S(1)}, u32[]{:S(2)}, u32[]{:S(2)}) collective-permute-start(f32[64,256]{1,0:T(8,128)S(1)} %get-tuple-element.30), channel_id=1, source_target_pairs={{0,1},{1,2},{2,3},{4,5},{5,6},{6,7},{8,9},{9,10},{10,11},{12,13},{... | collective-permute-start | bytes 196616 | tf_op jit(solution)/shard_map/ppermute | solution.py:200
  11.0 7.3 %collective-permute-start = (f32[64,128]{1,0:T(8,128)S(1)}, f32[64,128]{1,0:T(8,128)S(1)}, u32[]{:S(2)}, u32[]{:S(2)}) collective-permute-start(f32[64,128]{1,0:T(8,128)S(1)} %get-tuple-element.28), channel_id=1, source_target_pairs={{0,4},{4,8},{8,12},{12,16},{16,20},{20,24},{24,28},{28,0},{1,5},{5... | collective-permute-start | bytes 98312 | tf_op jit(solution)/shard_map/ppermute | solution.py:198
  13.4 4.9 %collective-permute-start.1 = (f32[64,128]{1,0:T(8,128)S(1)}, f32[64,128]{1,0:T(8,128)S(1)}, u32[]{:S(2)}, u32[]{:S(2)}) collective-permute-start(f32[64,128]{1,0:T(8,128)S(1)} %get-tuple-element.29), channel_id=1, source_target_pairs={{4,0},{8,4},{12,8},{16,12},{20,16},{24,20},{28,24},{0,28},{5,1},{9... | collective-permute-start | bytes 98312 | tf_op jit(solution)/shard_map/ppermute | solution.py:199
  16.5 0.7 %copy-start = (s32[6,256]{1,0:T(8,128)S(1)}, s32[6,256]{1,0:T(8,128)}, u32[]{:S(2)}) copy-start(s32[6,256]{1,0:T(8,128)} %links.19) | copy-start | bytes 18436
  17.2 10.3 %copy-start.1 = (s32[6,256]{1,0:T(8,128)S(1)}, s32[6,256]{1,0:T(8,128)}, u32[]{:S(2)}) copy-start(s32[6,256]{1,0:T(8,128)} %links.19) | copy-start | bytes 18436
  19.6 10.1 %collective-permute-start.5 = (f32[64,256]{1,0:T(8,128)S(1)}, f32[64,256]{1,0:T(8,128)S(1)}, u32[]{:S(2)}, u32[]{:S(2)}) collective-permute-start(f32[64,256]{1,0:T(8,128)S(1)} %get-tuple-element.36), channel_id=1, source_target_pairs={{0,1},{1,2},{2,3},{4,5},{5,6},{6,7},{8,9},{9,10},{10,11},{12,13},{... | collective-permute-start | bytes 196616 | tf_op jit(solution)/shard_map/ppermute | solution.py:200
  22.7 7.0 %collective-permute-start.3 = (f32[64,128]{1,0:T(8,128)S(1)}, f32[64,128]{1,0:T(8,128)S(1)}, u32[]{:S(2)}, u32[]{:S(2)}) collective-permute-start(f32[64,128]{1,0:T(8,128)S(1)} %get-tuple-element.34), channel_id=1, source_target_pairs={{0,4},{4,8},{8,12},{12,16},{16,20},{20,24},{24,28},{28,0},{1,5},{5... | collective-permute-start | bytes 98312 | tf_op jit(solution)/shard_map/ppermute | solution.py:198
  23.3 6.4 %collective-permute-start.4 = (f32[64,128]{1,0:T(8,128)S(1)}, f32[64,128]{1,0:T(8,128)S(1)}, u32[]{:S(2)}, u32[]{:S(2)}) collective-permute-start(f32[64,128]{1,0:T(8,128)S(1)} %get-tuple-element.35), channel_id=1, source_target_pairs={{4,0},{8,4},{12,8},{16,12},{20,16},{24,20},{28,24},{0,28},{5,1},{9... | collective-permute-start | bytes 98312 | tf_op jit(solution)/shard_map/ppermute | solution.py:199
  31.0 8.8 %collective-permute-start.8 = (f32[64,256]{1,0:T(8,128)S(1)}, f32[64,256]{1,0:T(8,128)S(1)}, u32[]{:S(2)}, u32[]{:S(2)}) collective-permute-start(f32[64,256]{1,0:T(8,128)S(1)} %get-tuple-element.40), channel_id=1, source_target_pairs={{0,1},{1,2},{2,3},{4,5},{5,6},{6,7},{8,9},{9,10},{10,11},{12,13},{... | collective-permute-start | bytes 196616 | tf_op jit(solution)/shard_map/ppermute | solution.py:200
  33.0 6.7 %collective-permute-start.6 = (f32[64,128]{1,0:T(8,128)S(1)}, f32[64,128]{1,0:T(8,128)S(1)}, u32[]{:S(2)}, u32[]{:S(2)}) collective-permute-start(f32[64,128]{1,0:T(8,128)S(1)} %get-tuple-element.38), channel_id=1, source_target_pairs={{0,4},{4,8},{8,12},{12,16},{16,20},{20,24},{24,28},{28,0},{1,5},{5... | collective-permute-start | bytes 98312 | tf_op jit(solution)/shard_map/ppermute | solution.py:198
  33.1 6.7 %collective-permute-start.7 = (f32[64,128]{1,0:T(8,128)S(1)}, f32[64,128]{1,0:T(8,128)S(1)}, u32[]{:S(2)}, u32[]{:S(2)}) collective-permute-start(f32[64,128]{1,0:T(8,128)S(1)} %get-tuple-element.39), channel_id=1, source_target_pairs={{4,0},{8,4},{12,8},{16,12},{20,16},{24,20},{28,24},{0,28},{5,1},{9... | collective-permute-start | bytes 98312 | tf_op jit(solution)/shard_map/ppermute | solution.py:199
  41.1 8.7 %collective-permute-start.11 = (f32[64,256]{1,0:T(8,128)S(1)}, f32[64,256]{1,0:T(8,128)S(1)}, u32[]{:S(2)}, u32[]{:S(2)}) collective-permute-start(f32[64,256]{1,0:T(8,128)S(1)} %get-tuple-element.44), channel_id=1, source_target_pairs={{0,1},{1,2},{2,3},{4,5},{5,6},{6,7},{8,9},{9,10},{10,11},{12,13},{... | collective-permute-start | bytes 196616 | tf_op jit(solution)/shard_map/ppermute | solution.py:200
  42.8 6.9 %collective-permute-start.9 = (f32[64,128]{1,0:T(8,128)S(1)}, f32[64,128]{1,0:T(8,128)S(1)}, u32[]{:S(2)}, u32[]{:S(2)}) collective-permute-start(f32[64,128]{1,0:T(8,128)S(1)} %get-tuple-element.42), channel_id=1, source_target_pairs={{0,4},{4,8},{8,12},{12,16},{16,20},{20,24},{24,28},{28,0},{1,5},{5... | collective-permute-start | bytes 98312 | tf_op jit(solution)/shard_map/ppermute | solution.py:198
  42.9 6.9 %collective-permute-start.10 = (f32[64,128]{1,0:T(8,128)S(1)}, f32[64,128]{1,0:T(8,128)S(1)}, u32[]{:S(2)}, u32[]{:S(2)}) collective-permute-start(f32[64,128]{1,0:T(8,128)S(1)} %get-tuple-element.43), channel_id=1, source_target_pairs={{4,0},{8,4},{12,8},{16,12},{20,16},{24,20},{28,24},{0,28},{5,1},{9... | collective-permute-start | bytes 98312 | tf_op jit(solution)/shard_map/ppermute | solution.py:199
  51.1 8.7 %collective-permute-start.14 = (f32[64,256]{1,0:T(8,128)S(1)}, f32[64,256]{1,0:T(8,128)S(1)}, u32[]{:S(2)}, u32[]{:S(2)}) collective-permute-start(f32[64,256]{1,0:T(8,128)S(1)} %get-tuple-element.48), channel_id=1, source_target_pairs={{0,1},{1,2},{2,3},{4,5},{5,6},{6,7},{8,9},{9,10},{10,11},{12,13},{... | collective-permute-start | bytes 196616 | tf_op jit(solution)/shard_map/ppermute | solution.py:200
  53.0 6.7 %collective-permute-start.12 = (f32[64,128]{1,0:T(8,128)S(1)}, f32[64,128]{1,0:T(8,128)S(1)}, u32[]{:S(2)}, u32[]{:S(2)}) collective-permute-start(f32[64,128]{1,0:T(8,128)S(1)} %get-tuple-element.46), channel_id=1, source_target_pairs={{0,4},{4,8},{8,12},{12,16},{16,20},{20,24},{24,28},{28,0},{1,5},{5... | collective-permute-start | bytes 98312 | tf_op jit(solution)/shard_map/ppermute | solution.py:198
  53.1 6.7 %collective-permute-start.13 = (f32[64,128]{1,0:T(8,128)S(1)}, f32[64,128]{1,0:T(8,128)S(1)}, u32[]{:S(2)}, u32[]{:S(2)}) collective-permute-start(f32[64,128]{1,0:T(8,128)S(1)} %get-tuple-element.47), channel_id=1, source_target_pairs={{4,0},{8,4},{12,8},{16,12},{20,16},{24,20},{28,24},{0,28},{5,1},{9... | collective-permute-start | bytes 98312 | tf_op jit(solution)/shard_map/ppermute | solution.py:199

commit v3 on v2

--- a/solution.py
+++ b/solution.py
@@ -10,6 +10,7 @@
 BF16 = jnp.bfloat16
 
 VMEM = pl.BlockSpec(memory_space=pltpu.VMEM)
+HBM = pl.BlockSpec(memory_space=pltpu.HBM)
 SMEM = pl.BlockSpec(memory_space=pltpu.SMEM)
 
 
@@ -74,36 +75,54 @@
     return jnp.where(iota((1, elems), 1) < counts_ref[0], 1.0, 0.0)
 
 
-def prepare(counts, first, source, initial, inverse, lift, lift_time, exports,
-            weight, base, table, top, low, high, rows_ref):
-    elems = source.shape[2]
+def fetch(sources, targets, sems):
+    copies = [pltpu.make_async_copy(a, b, sems.at[i]) for i, (a, b) in enumerate(zip(sources, targets))]
+    for copy in copies:
+        copy.start()
+    for copy in copies:
+        copy.wait()
+
+
+def inverse_parts(inverse):
     dup = iota((512, 256), 0)
     row_pick = one_hot((dup % 4) * 64 + dup // 8 == iota((512, 256), 1))
-    inv_hi, inv_lo = split(inverse[...])
-    inv_hi = mm(row_pick, inv_hi).astype(BF16)
-    inv_lo = mm(row_pick, inv_lo).astype(BF16)
-
-    def solve(x_hi, x_lo):
-        return mm(inv_hi, x_hi) + (mm(inv_hi, x_lo) + mm(inv_lo, x_hi))
-
+    inv_hi, inv_lo = split(inverse)
+    return mm(row_pick, inv_hi).astype(BF16), mm(row_pick, inv_lo).astype(BF16)
+
+
+def product(a, b):
+    return mm(a[0], b[0]) + (mm(a[0], b[1]) + mm(a[1], b[0]))
+
+
+def prepare(counts, first, source_hbm, initial_hbm, inverse_hbm, lift_time_hbm, exports_hbm,
+            base, table, top, low, high, source, initial, inverse, lift_time, exports, rows_ref, sems):
+    fetch(
+        (source_hbm, initial_hbm, inverse_hbm, lift_time_hbm, exports_hbm),
+        (source, initial, inverse, lift_time, exports),
+        sems,
+    )
+    elems = source.shape[2]
     start = initial[...] * jnp.where(first[0] > 0, 1.0, 0.0)
-    lt_hi, lt_lo = split(lift_time[...].T)
-    st_hi, st_lo = split(start)
-    rhs = source[0] + (mm(lt_hi, st_hi) + (mm(lt_hi, st_lo) + mm(lt_lo, st_hi)))
-    rows = solve(*split(rhs)) * live_of(counts, elems)
+    rhs = source[0] + product(split(lift_time[...].T), split(start))
+    rows = product(inverse_parts(inverse[...]), split(rhs)) * live_of(counts, elems)
     base[...] = rows
     publish(rows, rows_ref, exports[...], table, top, low, high)
 
+
+def fold_lifts(inverse_hbm, lift_hbm, lift_time_hbm, weight, inverse, lift, lift_time, sems):
+    fetch((inverse_hbm, lift_hbm, lift_time_hbm), (inverse, lift, lift_time), sems)
+    inv = inverse_parts(inverse[...])
     col = iota((384, 768), 1)
     want = ((col % 4) * 16 + (col // 8) % 16) * 6 + col // 128
     col_pick = one_hot(want == iota((384, 768), 0))
     l_hi, l_lo = split(lift[...])
     l_hi = mm(l_hi, col_pick).astype(BF16)
     l_lo = mm(l_lo, col_pick).astype(BF16)
-    w_hi, w_lo = split(solve(l_hi, l_lo))
+    w_hi, w_lo = split(product(inv, (l_hi, l_lo)))
     weight[0:512, 0:768] = w_hi
     weight[512:1024, 0:768] = w_lo
-    t_hi, t_lo = split(solve(jnp.concatenate([lt_hi, lt_hi], 1), jnp.concatenate([lt_lo, lt_lo], 1)))
+    time = lift_time[...].T
+    t_hi, t_lo = split(product(inv, split(jnp.concatenate([time, time], 1))))
     weight[0:512, 768:896] = t_hi
     weight[512:1024, 768:896] = t_lo
 
@@ -185,15 +204,34 @@
     rows_scratch = pltpu.VMEM((elems // 128, 512, 128), F32)
     nbr_scratch = pltpu.VMEM((896, elems), BF16)
 
-    weight, base, table, top, low, high = pl.pallas_call(
+    def copied(*arrays):
+        return [pltpu.VMEM(x.shape, x.dtype) for x in arrays]
+
+    lift_time = lift_time.T
+    source, initial, inverse, lift, lift_time, exports_in = (
+        pltpu.with_memory_space_constraint(x, pltpu.HBM)
+        for x in (source, initial, inverse, lift, lift_time, exports)
+    )
+    fetched = (source, initial, inverse, lift_time, exports_in)
+    base, table, top, low, high = pl.pallas_call(
         prepare,
-        out_shape=[S((1024, 896), BF16), S((512, elems), F32)] + published,
-        in_specs=[SMEM, SMEM] + [VMEM] * 6,
-        out_specs=[VMEM] * 6,
-        scratch_shapes=[rows_scratch],
+        out_shape=[S((512, elems), F32)] + published,
+        in_specs=[SMEM, SMEM] + [HBM] * 5,
+        out_specs=[VMEM] * 5,
+        scratch_shapes=copied(*fetched) + [rows_scratch, pltpu.SemaphoreType.DMA((5,))],
         compiler_params=params,
         name="prepare",
-    )(counts, first, source, initial, inverse, lift, lift_time.T, exports)
+    )(counts, first, *fetched)
+    fetched = (inverse, lift, lift_time)
+    weight = pl.pallas_call(
+        fold_lifts,
+        out_shape=S((1024, 896), BF16),
+        in_specs=[HBM] * 3,
+        out_specs=VMEM,
+        scratch_shapes=copied(*fetched) + [pltpu.SemaphoreType.DMA((3,))],
+        compiler_params=params,
+        name="fold_lifts",
+    )(*fetched)
     for step in range(1, ITERS):
         from_low = lax.ppermute(high, "space", up)
         from_high = lax.ppermute(low, "space", down)

time: 61.9 us -> 57.8 us (0.934)
  local copies, waits for them, and re-layouts: 5.95 us -> 0.02 us
  Pallas kernels: 13.5 us -> 15.9 us
  waiting for transfers between devices: 5.4 us -> 4.62 us
    unnamed x18 -> x6, local copies, waits for them, and re-layouts: 5.95 us -> 0.02 us
    pallas_call x1 -> x2, Pallas kernels: 2.64 us -> 5.04 us  [the longest x1 2.69 us: body(): pl.pallas_call(fold_lifts, out_shape=S((1024, 896), BF16), in_specs=[HBM]...]
    ppermute x5, starting transfers between devices: 21.4 us -> 22.4 us  [body(): from_high = lax.ppermute(low, 'space', down)]
    ppermute x5, waiting for transfers between devices: 5.38 us -> 4.59 us  [body(): from_low = lax.ppermute(high, 'space', up)]
  transfers between devices with their start and end apart: 15 -> 15, of which waited for: 5 -> 4; matrix products, arithmetic and copies ran while one was open for 0% -> 0% of each run, Pallas kernels for 6% -> 12%
where the time goes in v3:
time: 57.8 us; the launch traced here: 57.5 us
  starting transfers between devices  36.1 us (62%)
  Pallas kernels  15.9 us (28%)
  waiting for transfers between devices  4.62 us (8%)
  between operations  0.9 us (2%)
    ppermute x5, starting transfers between devices, body(): from_high = lax.ppermute(low, 'space', down)  22.4 us
    ppermute x5, starting transfers between devices, body(): top_in = lax.ppermute(top, 'slab', later)  11.1 us
    pallas_call x4, Pallas kernels, body(): pl.pallas_call(step_kernel, out_shape=published, in_specs=[SMEM] + [VMEM]...  5.18 us
    ppermute x5, waiting for transfers between devices, body(): from_low = lax.ppermute(high, 'space', up)  4.59 us
    pallas_call x5, Pallas kernels, body(): pl.pallas_call(gather_local, out_shape=S((128, 6 * elems), BF16), in_spec...  3.97 us
    pallas_call x1, Pallas kernels, body(): pl.pallas_call(fold_lifts, out_shape=S((1024, 896), BF16), in_specs=[HBM]...  2.69 us
    ppermute x5, starting transfers between devices, body(): from_low = lax.ppermute(high, 'space', up)  2.63 us
    pallas_call x1, Pallas kernels, body(): pl.pallas_call(prepare, out_shape=[S((512, elems), F32)] + published, in_...  2.35 us
  transfers between devices with their start and end apart: 15, of which 4 were waited for; matrix products, arithmetic and copies ran while one was open for 0% of the time, Pallas kernels for 12%

profile of v3, /device:TPU:0, one launch (start us, length us, event | category | flops | bytes accessed | tf_op | source)
XLA Modules:
  0.0 57.5 jit_solution(16508907068569531398)
XLA Ops:
  0.7 2.3 %prepare.1 = (f32[512,256]{1,0:T(8,128)S(1)}, bf16[128,1536]{1,0:T(8,128)(2,1)S(1)}, f32[64,256]{1,0:T(8,128)S(1)}, f32[64,128]{1,0:T(8,128)S(1)}, f32[64,128]{1,0:T(8,128)S(1)}) custom-call(s32[1]{0:T(128)S(6)} %copy.10.counts, s32[1]{0:T(128)} %bitcast.first, f32[1,256,256]{2,1,0:T(8,128)} %source_hbm.1, f32[64,256]{1,0:T(8,128)} %initial_hbm.1, ...), custom_call_target="tpu_custom_call" | custom-call | tf_op jit(solution)/shard_map/prepare/pallas_call | solution.py:216
  3.0 2.4 %collective-permute-start.2 = (f32[64,256]{1,0:T(8,128)S(1)}, f32[64,256]{1,0:T(8,128)S(1)}, u32[]{:S(2)}, u32[]{:S(2)}) collective-permute-start(f32[64,256]{1,0:T(8,128)S(1)} %get-tuple-element.29), channel_id=1, source_target_pairs={{0,1},{1,2},{2,3},{4,5},{5,6},{6,7},{8,9},{9,10},{10,11},{12,13},{... | collective-permute-start | bytes 196616 | tf_op jit(solution)/shard_map/ppermute | solution.py:238
  5.5 2.4 %collective-permute-start = (f32[64,128]{1,0:T(8,128)S(1)}, f32[64,128]{1,0:T(8,128)S(1)}, u32[]{:S(2)}, u32[]{:S(2)}) collective-permute-start(f32[64,128]{1,0:T(8,128)S(1)} %get-tuple-element.27), channel_id=1, source_target_pairs={{0,4},{4,8},{8,12},{12,16},{16,20},{20,24},{24,28},{28,0},{1,5},{5... | collective-permute-start | bytes 98312 | tf_op jit(solution)/shard_map/ppermute | solution.py:236
  7.8 3.1 %collective-permute-start.1 = (f32[64,128]{1,0:T(8,128)S(1)}, f32[64,128]{1,0:T(8,128)S(1)}, u32[]{:S(2)}, u32[]{:S(2)}) collective-permute-start(f32[64,128]{1,0:T(8,128)S(1)} %get-tuple-element.28), channel_id=1, source_target_pairs={{4,0},{8,4},{12,8},{16,12},{20,16},{24,20},{28,24},{0,28},{5,1},{9... | collective-permute-start | bytes 98312 | tf_op jit(solution)/shard_map/ppermute | solution.py:237
  10.9 2.7 %fold_lifts.1.weight = bf16[1024,896]{1,0:T(8,128)(2,1)S(1)} custom-call(f32[256,256]{1,0:T(8,128)} %inverse_hbm.3, f32[256,384]{1,0:T(8,128)} %lift_hbm.1, f32[64,256]{1,0:T(8,128)} %bitcast.9), custom_call_target="tpu_custom_call" | custom-call | tf_op jit(solution)/shard_map/fold_lifts/pallas_call | solution.py:226
  13.6 0.8 %gather_local.5.local = bf16[128,1536]{1,0:T(8,128)(2,1)S(1)} custom-call(bf16[128,1536]{1,0:T(8,128)(2,1)S(1)} %get-tuple-element.26.table, s32[6,256]{1,0:T(8,128)S(1)} %copy-done), custom_call_target="tpu_custom_call" | custom-call | tf_op jit(solution)/shard_map/gather_local/pallas_call | solution.py:239
  14.5 1.3 %advance.4 = (bf16[128,1536]{1,0:T(8,128)(2,1)S(1)}, f32[64,256]{1,0:T(8,128)S(1)}, f32[64,128]{1,0:T(8,128)S(1)}, f32[64,128]{1,0:T(8,128)S(1)}) custom-call(s32[1]{0:T(128)S(6)} %copy.10.counts, bf16[128,1536]{1,0:T(8,128)(2,1)S(1)} %gather_local.5.local, f32[64,128]{1,0:T(8,128)S(1)} %collective-permute-done.from_low, ...), custom_call_target="tpu_custom_call" | custom-call | tf_op jit(solution)/shard_map/advance/pallas_call | solution.py:252
  15.8 3.4 %collective-permute-start.5 = (f32[64,256]{1,0:T(8,128)S(1)}, f32[64,256]{1,0:T(8,128)S(1)}, u32[]{:S(2)}, u32[]{:S(2)}) collective-permute-start(f32[64,256]{1,0:T(8,128)S(1)} %get-tuple-element.34), channel_id=1, source_target_pairs={{0,1},{1,2},{2,3},{4,5},{5,6},{6,7},{8,9},{9,10},{10,11},{12,13},{... | collective-permute-start | bytes 196616 | tf_op jit(solution)/shard_map/ppermute | solution.py:238
  19.3 4.7 %collective-permute-start.4 = (f32[64,128]{1,0:T(8,128)S(1)}, f32[64,128]{1,0:T(8,128)S(1)}, u32[]{:S(2)}, u32[]{:S(2)}) collective-permute-start(f32[64,128]{1,0:T(8,128)S(1)} %get-tuple-element.33), channel_id=1, source_target_pairs={{4,0},{8,4},{12,8},{16,12},{20,16},{24,20},{28,24},{0,28},{5,1},{9... | collective-permute-start | bytes 98312 | tf_op jit(solution)/shard_map/ppermute | solution.py:237
  24.0 0.8 %gather_local.6.local = bf16[128,1536]{1,0:T(8,128)(2,1)S(1)} custom-call(bf16[128,1536]{1,0:T(8,128)(2,1)S(1)} %get-tuple-element.31.table, s32[6,256]{1,0:T(8,128)S(1)} %copy-done), custom_call_target="tpu_custom_call" | custom-call | tf_op jit(solution)/shard_map/gather_local/pallas_call | solution.py:239
  24.8 1.1 %collective-permute-done.3.from_low = f32[64,128]{1,0:T(8,128)S(1)} collective-permute-done((f32[64,128]{1,0:T(8,128)S(1)}, f32[64,128]{1,0:T(8,128)S(1)}, u32[]{:S(2)}, u32[]{:S(2)}) %collective-permute-start.3) | collective-permute-done | bytes 32800 | tf_op jit(solution)/shard_map/ppermute | solution.py:236
  25.9 1.3 %advance.5 = (bf16[128,1536]{1,0:T(8,128)(2,1)S(1)}, f32[64,256]{1,0:T(8,128)S(1)}, f32[64,128]{1,0:T(8,128)S(1)}, f32[64,128]{1,0:T(8,128)S(1)}) custom-call(s32[1]{0:T(128)S(6)} %copy.10.counts, bf16[128,1536]{1,0:T(8,128)(2,1)S(1)} %gather_local.6.local, f32[64,128]{1,0:T(8,128)S(1)} %collective-permute-done.3.from_low, ...), custom_call_target="tpu_custom_call" | custom-call | tf_op jit(solution)/shard_map/advance/pallas_call | solution.py:252
  27.2 1.3 %collective-permute-start.8 = (f32[64,256]{1,0:T(8,128)S(1)}, f32[64,256]{1,0:T(8,128)S(1)}, u32[]{:S(2)}, u32[]{:S(2)}) collective-permute-start(f32[64,256]{1,0:T(8,128)S(1)} %get-tuple-element.38), channel_id=1, source_target_pairs={{0,1},{1,2},{2,3},{4,5},{5,6},{6,7},{8,9},{9,10},{10,11},{12,13},{... | collective-permute-start | bytes 196616 | tf_op jit(solution)/shard_map/ppermute | solution.py:238
  28.6 4.8 %collective-permute-start.7 = (f32[64,128]{1,0:T(8,128)S(1)}, f32[64,128]{1,0:T(8,128)S(1)}, u32[]{:S(2)}, u32[]{:S(2)}) collective-permute-start(f32[64,128]{1,0:T(8,128)S(1)} %get-tuple-element.37), channel_id=1, source_target_pairs={{4,0},{8,4},{12,8},{16,12},{20,16},{24,20},{28,24},{0,28},{5,1},{9... | collective-permute-start | bytes 98312 | tf_op jit(solution)/shard_map/ppermute | solution.py:237
  34.1 1.1 %collective-permute-done.6.from_low = f32[64,128]{1,0:T(8,128)S(1)} collective-permute-done((f32[64,128]{1,0:T(8,128)S(1)}, f32[64,128]{1,0:T(8,128)S(1)}, u32[]{:S(2)}, u32[]{:S(2)}) %collective-permute-start.6) | collective-permute-done | bytes 32800 | tf_op jit(solution)/shard_map/ppermute | solution.py:236
  35.2 1.3 %advance.6 = (bf16[128,1536]{1,0:T(8,128)(2,1)S(1)}, f32[64,256]{1,0:T(8,128)S(1)}, f32[64,128]{1,0:T(8,128)S(1)}, f32[64,128]{1,0:T(8,128)S(1)}) custom-call(s32[1]{0:T(128)S(6)} %copy.10.counts, bf16[128,1536]{1,0:T(8,128)(2,1)S(1)} %gather_local.7.local, f32[64,128]{1,0:T(8,128)S(1)} %collective-permute-done.6.from_low, ...), custom_call_target="tpu_custom_call" | custom-call | tf_op jit(solution)/shard_map/advance/pallas_call | solution.py:252
  36.5 2.1 %collective-permute-start.11 = (f32[64,256]{1,0:T(8,128)S(1)}, f32[64,256]{1,0:T(8,128)S(1)}, u32[]{:S(2)}, u32[]{:S(2)}) collective-permute-start(f32[64,256]{1,0:T(8,128)S(1)} %get-tuple-element.42), channel_id=1, source_target_pairs={{0,1},{1,2},{2,3},{4,5},{5,6},{6,7},{8,9},{9,10},{10,11},{12,13},{... | collective-permute-start | bytes 196616 | tf_op jit(solution)/shard_map/ppermute | solution.py:238
  38.6 5.1 %collective-permute-start.10 = (f32[64,128]{1,0:T(8,128)S(1)}, f32[64,128]{1,0:T(8,128)S(1)}, u32[]{:S(2)}, u32[]{:S(2)}) collective-permute-start(f32[64,128]{1,0:T(8,128)S(1)} %get-tuple-element.41), channel_id=1, source_target_pairs={{4,0},{8,4},{12,8},{16,12},{20,16},{24,20},{28,24},{0,28},{5,1},{9... | collective-permute-start | bytes 98312 | tf_op jit(solution)/shard_map/ppermute | solution.py:237
  44.5 1.3 %collective-permute-done.9.from_low = f32[64,128]{1,0:T(8,128)S(1)} collective-permute-done((f32[64,128]{1,0:T(8,128)S(1)}, f32[64,128]{1,0:T(8,128)S(1)}, u32[]{:S(2)}, u32[]{:S(2)}) %collective-permute-start.9) | collective-permute-done | bytes 32800 | tf_op jit(solution)/shard_map/ppermute | solution.py:236
  45.8 1.3 %advance.7 = (bf16[128,1536]{1,0:T(8,128)(2,1)S(1)}, f32[64,256]{1,0:T(8,128)S(1)}, f32[64,128]{1,0:T(8,128)S(1)}, f32[64,128]{1,0:T(8,128)S(1)}) custom-call(s32[1]{0:T(128)S(6)} %copy.10.counts, bf16[128,1536]{1,0:T(8,128)(2,1)S(1)} %gather_local.8.local, f32[64,128]{1,0:T(8,128)S(1)} %collective-permute-done.9.from_low, ...), custom_call_target="tpu_custom_call" | custom-call | tf_op jit(solution)/shard_map/advance/pallas_call | solution.py:252
  47.1 1.9 %collective-permute-start.14 = (f32[64,256]{1,0:T(8,128)S(1)}, f32[64,256]{1,0:T(8,128)S(1)}, u32[]{:S(2)}, u32[]{:S(2)}) collective-permute-start(f32[64,256]{1,0:T(8,128)S(1)} %get-tuple-element.46), channel_id=1, source_target_pairs={{0,1},{1,2},{2,3},{4,5},{5,6},{6,7},{8,9},{9,10},{10,11},{12,13},{... | collective-permute-start | bytes 196616 | tf_op jit(solution)/shard_map/ppermute | solution.py:238
  49.1 4.7 %collective-permute-start.13 = (f32[64,128]{1,0:T(8,128)S(1)}, f32[64,128]{1,0:T(8,128)S(1)}, u32[]{:S(2)}, u32[]{:S(2)}) collective-permute-start(f32[64,128]{1,0:T(8,128)S(1)} %get-tuple-element.45), channel_id=1, source_target_pairs={{4,0},{8,4},{12,8},{16,12},{20,16},{24,20},{28,24},{0,28},{5,1},{9... | collective-permute-start | bytes 98312 | tf_op jit(solution)/shard_map/ppermute | solution.py:237
  54.6 1.2 %collective-permute-done.12.from_low = f32[64,128]{1,0:T(8,128)S(1)} collective-permute-done((f32[64,128]{1,0:T(8,128)S(1)}, f32[64,128]{1,0:T(8,128)S(1)}, u32[]{:S(2)}, u32[]{:S(2)}) %collective-permute-start.12) | collective-permute-done | bytes 32800 | tf_op jit(solution)/shard_map/ppermute | solution.py:236
  55.8 1.7 %advance_last.1 = f32[1,256,256]{2,1,0:T(8,128)} custom-call(s32[1]{0:T(128)S(6)} %copy.10.counts, bf16[128,1536]{1,0:T(8,128)(2,1)S(1)} %gather_local.9.local, f32[64,128]{1,0:T(8,128)S(1)} %collective-permute-done.12.from_low, f32[64,128]{1,0:T(8,128)S(1)} %collective-permute-done.13.from_high, f32[64,256]{1,0:T(8,128)S(1)} %collective-permute-done.14.top_in, ...), custom_call_target="tpu_custom_call" | custom-call | tf_op jit(solution)/shard_map/advance_last/pallas_call | solution.py:262
  (24 shorter events, 2.7 us)
Async XLA Ops:
  0.0 13.6 %copy-start = (s32[6,256]{1,0:T(8,128)S(1)}, s32[6,256]{1,0:T(8,128)}, u32[]{:S(2)}) copy-start(s32[6,256]{1,0:T(8,128)} %links.19) | copy-start | bytes 18436
  3.0 11.5 %copy-start.1 = (s32[6,256]{1,0:T(8,128)S(1)}, s32[6,256]{1,0:T(8,128)}, u32[]{:S(2)}) copy-start(s32[6,256]{1,0:T(8,128)} %orient.9) | copy-start | bytes 18436
  3.0 11.5 %copy-start.2 = (s32[256]{0:T(256)S(1)}, s32[256]{0:T(256)}, u32[]{:S(2)}) copy-start(s32[256]{0:T(256)} %param.16) | copy-start | bytes 3076
  3.0 11.4 %collective-permute-start.2 = (f32[64,256]{1,0:T(8,128)S(1)}, f32[64,256]{1,0:T(8,128)S(1)}, u32[]{:S(2)}, u32[]{:S(2)}) collective-permute-start(f32[64,256]{1,0:T(8,128)S(1)} %get-tuple-element.29), channel_id=1, source_target_pairs={{0,1},{1,2},{2,3},{4,5},{5,6},{6,7},{8,9},{9,10},{10,11},{12,13},{... | collective-permute-start | bytes 196616 | tf_op jit(solution)/shard_map/ppermute | solution.py:238
  5.5 9.0 %collective-permute-start = (f32[64,128]{1,0:T(8,128)S(1)}, f32[64,128]{1,0:T(8,128)S(1)}, u32[]{:S(2)}, u32[]{:S(2)}) collective-permute-start(f32[64,128]{1,0:T(8,128)S(1)} %get-tuple-element.27), channel_id=1, source_target_pairs={{0,4},{4,8},{8,12},{12,16},{16,20},{20,24},{24,28},{28,0},{1,5},{5... | collective-permute-start | bytes 98312 | tf_op jit(solution)/shard_map/ppermute | solution.py:236
  7.8 6.6 %collective-permute-start.1 = (f32[64,128]{1,0:T(8,128)S(1)}, f32[64,128]{1,0:T(8,128)S(1)}, u32[]{:S(2)}, u32[]{:S(2)}) collective-permute-start(f32[64,128]{1,0:T(8,128)S(1)} %get-tuple-element.28), channel_id=1, source_target_pairs={{4,0},{8,4},{12,8},{16,12},{20,16},{24,20},{28,24},{0,28},{5,1},{9... | collective-permute-start | bytes 98312 | tf_op jit(solution)/shard_map/ppermute | solution.py:237
  15.8 10.1 %collective-permute-start.5 = (f32[64,256]{1,0:T(8,128)S(1)}, f32[64,256]{1,0:T(8,128)S(1)}, u32[]{:S(2)}, u32[]{:S(2)}) collective-permute-start(f32[64,256]{1,0:T(8,128)S(1)} %get-tuple-element.34), channel_id=1, source_target_pairs={{0,1},{1,2},{2,3},{4,5},{5,6},{6,7},{8,9},{9,10},{10,11},{12,13},{... | collective-permute-start | bytes 196616 | tf_op jit(solution)/shard_map/ppermute | solution.py:238
  19.2 6.7 %collective-permute-start.3 = (f32[64,128]{1,0:T(8,128)S(1)}, f32[64,128]{1,0:T(8,128)S(1)}, u32[]{:S(2)}, u32[]{:S(2)}) collective-permute-start(f32[64,128]{1,0:T(8,128)S(1)} %get-tuple-element.32), channel_id=1, source_target_pairs={{0,4},{4,8},{8,12},{12,16},{16,20},{20,24},{24,28},{28,0},{1,5},{5... | collective-permute-start | bytes 98312 | tf_op jit(solution)/shard_map/ppermute | solution.py:236
  19.3 6.6 %collective-permute-start.4 = (f32[64,128]{1,0:T(8,128)S(1)}, f32[64,128]{1,0:T(8,128)S(1)}, u32[]{:S(2)}, u32[]{:S(2)}) collective-permute-start(f32[64,128]{1,0:T(8,128)S(1)} %get-tuple-element.33), channel_id=1, source_target_pairs={{4,0},{8,4},{12,8},{16,12},{20,16},{24,20},{28,24},{0,28},{5,1},{9... | collective-permute-start | bytes 98312 | tf_op jit(solution)/shard_map/ppermute | solution.py:237
  27.2 8.0 %collective-permute-start.8 = (f32[64,256]{1,0:T(8,128)S(1)}, f32[64,256]{1,0:T(8,128)S(1)}, u32[]{:S(2)}, u32[]{:S(2)}) collective-permute-start(f32[64,256]{1,0:T(8,128)S(1)} %get-tuple-element.38), channel_id=1, source_target_pairs={{0,1},{1,2},{2,3},{4,5},{5,6},{6,7},{8,9},{9,10},{10,11},{12,13},{... | collective-permute-start | bytes 196616 | tf_op jit(solution)/shard_map/ppermute | solution.py:238
  28.5 6.7 %collective-permute-start.6 = (f32[64,128]{1,0:T(8,128)S(1)}, f32[64,128]{1,0:T(8,128)S(1)}, u32[]{:S(2)}, u32[]{:S(2)}) collective-permute-start(f32[64,128]{1,0:T(8,128)S(1)} %get-tuple-element.36), channel_id=1, source_target_pairs={{0,4},{4,8},{8,12},{12,16},{16,20},{20,24},{24,28},{28,0},{1,5},{5... | collective-permute-start | bytes 98312 | tf_op jit(solution)/shard_map/ppermute | solution.py:236
  28.6 6.6 %collective-permute-start.7 = (f32[64,128]{1,0:T(8,128)S(1)}, f32[64,128]{1,0:T(8,128)S(1)}, u32[]{:S(2)}, u32[]{:S(2)}) collective-permute-start(f32[64,128]{1,0:T(8,128)S(1)} %get-tuple-element.37), channel_id=1, source_target_pairs={{4,0},{8,4},{12,8},{16,12},{20,16},{24,20},{28,24},{0,28},{5,1},{9... | collective-permute-start | bytes 98312 | tf_op jit(solution)/shard_map/ppermute | solution.py:237
  36.5 9.3 %collective-permute-start.11 = (f32[64,256]{1,0:T(8,128)S(1)}, f32[64,256]{1,0:T(8,128)S(1)}, u32[]{:S(2)}, u32[]{:S(2)}) collective-permute-start(f32[64,256]{1,0:T(8,128)S(1)} %get-tuple-element.42), channel_id=1, source_target_pairs={{0,1},{1,2},{2,3},{4,5},{5,6},{6,7},{8,9},{9,10},{10,11},{12,13},{... | collective-permute-start | bytes 196616 | tf_op jit(solution)/shard_map/ppermute | solution.py:238
  38.6 7.2 %collective-permute-start.9 = (f32[64,128]{1,0:T(8,128)S(1)}, f32[64,128]{1,0:T(8,128)S(1)}, u32[]{:S(2)}, u32[]{:S(2)}) collective-permute-start(f32[64,128]{1,0:T(8,128)S(1)} %get-tuple-element.40), channel_id=1, source_target_pairs={{0,4},{4,8},{8,12},{12,16},{16,20},{20,24},{24,28},{28,0},{1,5},{5... | collective-permute-start | bytes 98312 | tf_op jit(solution)/shard_map/ppermute | solution.py:236
  38.6 7.2 %collective-permute-start.10 = (f32[64,128]{1,0:T(8,128)S(1)}, f32[64,128]{1,0:T(8,128)S(1)}, u32[]{:S(2)}, u32[]{:S(2)}) collective-permute-start(f32[64,128]{1,0:T(8,128)S(1)} %get-tuple-element.41), channel_id=1, source_target_pairs={{4,0},{8,4},{12,8},{16,12},{20,16},{24,20},{28,24},{0,28},{5,1},{9... | collective-permute-start | bytes 98312 | tf_op jit(solution)/shard_map/ppermute | solution.py:237
  47.1 8.7 %collective-permute-start.14 = (f32[64,256]{1,0:T(8,128)S(1)}, f32[64,256]{1,0:T(8,128)S(1)}, u32[]{:S(2)}, u32[]{:S(2)}) collective-permute-start(f32[64,256]{1,0:T(8,128)S(1)} %get-tuple-element.46), channel_id=1, source_target_pairs={{0,1},{1,2},{2,3},{4,5},{5,6},{6,7},{8,9},{9,10},{10,11},{12,13},{... | collective-permute-start | bytes 196616 | tf_op jit(solution)/shard_map/ppermute | solution.py:238
  49.1 6.7 %collective-permute-start.12 = (f32[64,128]{1,0:T(8,128)S(1)}, f32[64,128]{1,0:T(8,128)S(1)}, u32[]{:S(2)}, u32[]{:S(2)}) collective-permute-start(f32[64,128]{1,0:T(8,128)S(1)} %get-tuple-element.44), channel_id=1, source_target_pairs={{0,4},{4,8},{8,12},{12,16},{16,20},{20,24},{24,28},{28,0},{1,5},{5... | collective-permute-start | bytes 98312 | tf_op jit(solution)/shard_map/ppermute | solution.py:236
  49.1 6.7 %collective-permute-start.13 = (f32[64,128]{1,0:T(8,128)S(1)}, f32[64,128]{1,0:T(8,128)S(1)}, u32[]{:S(2)}, u32[]{:S(2)}) collective-permute-start(f32[64,128]{1,0:T(8,128)S(1)} %get-tuple-element.45), channel_id=1, source_target_pairs={{4,0},{8,4},{12,8},{16,12},{20,16},{24,20},{28,24},{0,28},{5,1},{9... | collective-permute-start | bytes 98312 | tf_op jit(solution)/shard_map/ppermute | solution.py:237

commit v4 on v3

--- a/solution.py
+++ b/solution.py
@@ -235,7 +235,6 @@
     for step in range(1, ITERS):
         from_low = lax.ppermute(high, "space", up)
         from_high = lax.ppermute(low, "space", down)
-        top_in = lax.ppermute(top, "slab", later)
         local = pl.pallas_call(
             gather_local,
             out_shape=S((128, 6 * elems), BF16),
@@ -244,6 +243,8 @@
             compiler_params=params,
             name="gather_local",
         )(table, links)
+        top, local = lax.optimization_barrier((top, local))
+        top_in = lax.ppermute(top, "slab", later)
         from_low, from_high, top_in = (
             pltpu.with_memory_space_constraint(x, pltpu.VMEM) for x in (from_low, from_high, top_in)
         )

time: 57.8 us -> 61.6 us (1.066)
  waiting for transfers between devices: 4.62 us -> 7.8 us
  local copies, waits for them, and re-layouts: 0.02 us -> 0.71 us
    ppermute x5, waiting for transfers between devices: 4.59 us -> 7.77 us  [body(): from_low = lax.ppermute(high, 'space', up)]
    unnamed x6, local copies, waits for them, and re-layouts: 0.02 us -> 0.71 us
  transfers between devices with their start and end apart: 15 -> 15, of which waited for: 4 -> 4; matrix products, arithmetic and copies ran while one was open for 0% -> 0% of each run, Pallas kernels for 12% -> 4%
where the time goes in v4:
time: 61.6 us; the launch traced here: 61.3 us
  starting transfers between devices  36.1 us (59%)
  Pallas kernels  15.9 us (26%)
  waiting for transfers between devices  7.8 us (13%)
  between operations  0.88 us (1%)
  local copies, waits for them, and re-layouts  0.71 us (1%)
    ppermute x5, starting transfers between devices, body(): from_high = lax.ppermute(low, 'space', down)  22.4 us
    ppermute x5, starting transfers between devices, body(): top_in = lax.ppermute(top, 'slab', later)  11.1 us
    ppermute x5, waiting for transfers between devices, body(): from_low = lax.ppermute(high, 'space', up)  7.77 us
    pallas_call x4, Pallas kernels, body(): pl.pallas_call(step_kernel, out_shape=published, in_specs=[SMEM] + [VMEM]...  5.19 us
    pallas_call x5, Pallas kernels, body(): pl.pallas_call(gather_local, out_shape=S((128, 6 * elems), BF16), in_spec...  3.96 us
    pallas_call x1, Pallas kernels, body(): pl.pallas_call(fold_lifts, out_shape=S((1024, 896), BF16), in_specs=[HBM]...  2.69 us
    ppermute x5, starting transfers between devices, body(): from_low = lax.ppermute(high, 'space', up)  2.63 us
    pallas_call x1, Pallas kernels, body(): pl.pallas_call(prepare, out_shape=[S((512, elems), F32)] + published, in_...  2.35 us
  transfers between devices with their start and end apart: 15, of which 4 were waited for; matrix products, arithmetic and copies ran while one was open for 0% of the time, Pallas kernels for 4%

profile of v4, /device:TPU:0, one launch (start us, length us, event | category | flops | bytes accessed | tf_op | source)
XLA Modules:
  0.0 61.3 jit_solution(8409150001142004276)
XLA Ops:
  0.7 2.3 %prepare.1 = (f32[512,256]{1,0:T(8,128)S(1)}, bf16[128,1536]{1,0:T(8,128)(2,1)S(1)}, f32[64,256]{1,0:T(8,128)S(1)}, f32[64,128]{1,0:T(8,128)S(1)}, f32[64,128]{1,0:T(8,128)S(1)}) custom-call(s32[1]{0:T(128)S(6)} %copy.10.counts, s32[1]{0:T(128)} %bitcast.first, f32[1,256,256]{2,1,0:T(8,128)} %source_hbm.1, f32[64,256]{1,0:T(8,128)} %initial_hbm.1, ...), custom_call_target="tpu_custom_call" | custom-call | tf_op jit(solution)/shard_map/prepare/pallas_call | solution.py:216
  4.5 2.4 %collective-permute-start.2 = (f32[64,256]{1,0:T(8,128)S(1)}, f32[64,256]{1,0:T(8,128)S(1)}, u32[]{:S(2)}, u32[]{:S(2)}) collective-permute-start(f32[64,256]{1,0:T(8,128)S(1)} %get-tuple-element.41), channel_id=1, source_target_pairs={{0,1},{1,2},{2,3},{4,5},{5,6},{6,7},{8,9},{9,10},{10,11},{12,13},{... | collective-permute-start | bytes 196616 | tf_op jit(solution)/shard_map/ppermute | solution.py:247
  6.9 2.4 %collective-permute-start = (f32[64,128]{1,0:T(8,128)S(1)}, f32[64,128]{1,0:T(8,128)S(1)}, u32[]{:S(2)}, u32[]{:S(2)}) collective-permute-start(f32[64,128]{1,0:T(8,128)S(1)} %get-tuple-element.39), channel_id=1, source_target_pairs={{0,4},{4,8},{8,12},{12,16},{16,20},{20,24},{24,28},{28,0},{1,5},{5... | collective-permute-start | bytes 98312 | tf_op jit(solution)/shard_map/ppermute | solution.py:236
  9.3 3.1 %collective-permute-start.1 = (f32[64,128]{1,0:T(8,128)S(1)}, f32[64,128]{1,0:T(8,128)S(1)}, u32[]{:S(2)}, u32[]{:S(2)}) collective-permute-start(f32[64,128]{1,0:T(8,128)S(1)} %get-tuple-element.40), channel_id=1, source_target_pairs={{4,0},{8,4},{12,8},{16,12},{20,16},{24,20},{28,24},{0,28},{5,1},{9... | collective-permute-start | bytes 98312 | tf_op jit(solution)/shard_map/ppermute | solution.py:237
  12.4 2.7 %fold_lifts.1.weight = bf16[1024,896]{1,0:T(8,128)(2,1)S(1)} custom-call(f32[256,256]{1,0:T(8,128)} %inverse_hbm.3, f32[256,384]{1,0:T(8,128)} %lift_hbm.1, f32[64,256]{1,0:T(8,128)} %bitcast.9), custom_call_target="tpu_custom_call" | custom-call | tf_op jit(solution)/shard_map/fold_lifts/pallas_call | solution.py:226
  15.2 1.3 %advance.4 = (bf16[128,1536]{1,0:T(8,128)(2,1)S(1)}, f32[64,256]{1,0:T(8,128)S(1)}, f32[64,128]{1,0:T(8,128)S(1)}, f32[64,128]{1,0:T(8,128)S(1)}) custom-call(s32[1]{0:T(128)S(6)} %copy.10.counts, bf16[128,1536]{1,0:T(8,128)(2,1)S(1)} %gather_local.5.local, f32[64,128]{1,0:T(8,128)S(1)} %collective-permute-done.from_low, ...), custom_call_target="tpu_custom_call" | custom-call | tf_op jit(solution)/shard_map/advance/pallas_call | solution.py:253
  16.5 0.8 %gather_local.6.local = bf16[128,1536]{1,0:T(8,128)(2,1)S(1)} custom-call(bf16[128,1536]{1,0:T(8,128)(2,1)S(1)} %get-tuple-element.44.table, s32[6,256]{1,0:T(8,128)S(1)} %copy-done), custom_call_target="tpu_custom_call" | custom-call | tf_op jit(solution)/shard_map/gather_local/pallas_call | solution.py:238
  17.3 3.4 %collective-permute-start.5 = (f32[64,256]{1,0:T(8,128)S(1)}, f32[64,256]{1,0:T(8,128)S(1)}, u32[]{:S(2)}, u32[]{:S(2)}) collective-permute-start(f32[64,256]{1,0:T(8,128)S(1)} %get-tuple-element.48), channel_id=1, source_target_pairs={{0,1},{1,2},{2,3},{4,5},{5,6},{6,7},{8,9},{9,10},{10,11},{12,13},{... | collective-permute-start | bytes 196616 | tf_op jit(solution)/shard_map/ppermute | solution.py:247
  20.8 4.7 %collective-permute-start.4 = (f32[64,128]{1,0:T(8,128)S(1)}, f32[64,128]{1,0:T(8,128)S(1)}, u32[]{:S(2)}, u32[]{:S(2)}) collective-permute-start(f32[64,128]{1,0:T(8,128)S(1)} %get-tuple-element.47), channel_id=1, source_target_pairs={{4,0},{8,4},{12,8},{16,12},{20,16},{24,20},{28,24},{0,28},{5,1},{9... | collective-permute-start | bytes 98312 | tf_op jit(solution)/shard_map/ppermute | solution.py:237
  25.5 1.9 %collective-permute-done.3.from_low = f32[64,128]{1,0:T(8,128)S(1)} collective-permute-done((f32[64,128]{1,0:T(8,128)S(1)}, f32[64,128]{1,0:T(8,128)S(1)}, u32[]{:S(2)}, u32[]{:S(2)}) %collective-permute-start.3) | collective-permute-done | bytes 32800 | tf_op jit(solution)/shard_map/ppermute | solution.py:236
  27.4 1.3 %advance.5 = (bf16[128,1536]{1,0:T(8,128)(2,1)S(1)}, f32[64,256]{1,0:T(8,128)S(1)}, f32[64,128]{1,0:T(8,128)S(1)}, f32[64,128]{1,0:T(8,128)S(1)}) custom-call(s32[1]{0:T(128)S(6)} %copy.10.counts, bf16[128,1536]{1,0:T(8,128)(2,1)S(1)} %gather_local.6.local, f32[64,128]{1,0:T(8,128)S(1)} %collective-permute-done.3.from_low, ...), custom_call_target="tpu_custom_call" | custom-call | tf_op jit(solution)/shard_map/advance/pallas_call | solution.py:253
  29.5 1.3 %collective-permute-start.8 = (f32[64,256]{1,0:T(8,128)S(1)}, f32[64,256]{1,0:T(8,128)S(1)}, u32[]{:S(2)}, u32[]{:S(2)}) collective-permute-start(f32[64,256]{1,0:T(8,128)S(1)} %get-tuple-element.54), channel_id=1, source_target_pairs={{0,1},{1,2},{2,3},{4,5},{5,6},{6,7},{8,9},{9,10},{10,11},{12,13},{... | collective-permute-start | bytes 196616 | tf_op jit(solution)/shard_map/ppermute | solution.py:247
  30.8 4.8 %collective-permute-start.7 = (f32[64,128]{1,0:T(8,128)S(1)}, f32[64,128]{1,0:T(8,128)S(1)}, u32[]{:S(2)}, u32[]{:S(2)}) collective-permute-start(f32[64,128]{1,0:T(8,128)S(1)} %get-tuple-element.53), channel_id=1, source_target_pairs={{4,0},{8,4},{12,8},{16,12},{20,16},{24,20},{28,24},{0,28},{5,1},{9... | collective-permute-start | bytes 98312 | tf_op jit(solution)/shard_map/ppermute | solution.py:237
  35.6 1.8 %collective-permute-done.6.from_low = f32[64,128]{1,0:T(8,128)S(1)} collective-permute-done((f32[64,128]{1,0:T(8,128)S(1)}, f32[64,128]{1,0:T(8,128)S(1)}, u32[]{:S(2)}, u32[]{:S(2)}) %collective-permute-start.6) | collective-permute-done | bytes 32800 | tf_op jit(solution)/shard_map/ppermute | solution.py:236
  37.5 1.3 %advance.6 = (bf16[128,1536]{1,0:T(8,128)(2,1)S(1)}, f32[64,256]{1,0:T(8,128)S(1)}, f32[64,128]{1,0:T(8,128)S(1)}, f32[64,128]{1,0:T(8,128)S(1)}) custom-call(s32[1]{0:T(128)S(6)} %copy.10.counts, bf16[128,1536]{1,0:T(8,128)(2,1)S(1)} %gather_local.7.local, f32[64,128]{1,0:T(8,128)S(1)} %collective-permute-done.6.from_low, ...), custom_call_target="tpu_custom_call" | custom-call | tf_op jit(solution)/shard_map/advance/pallas_call | solution.py:253
  39.6 2.1 %collective-permute-start.11 = (f32[64,256]{1,0:T(8,128)S(1)}, f32[64,256]{1,0:T(8,128)S(1)}, u32[]{:S(2)}, u32[]{:S(2)}) collective-permute-start(f32[64,256]{1,0:T(8,128)S(1)} %get-tuple-element.60), channel_id=1, source_target_pairs={{0,1},{1,2},{2,3},{4,5},{5,6},{6,7},{8,9},{9,10},{10,11},{12,13},{... | collective-permute-start | bytes 196616 | tf_op jit(solution)/shard_map/ppermute | solution.py:247
  41.7 5.1 %collective-permute-start.10 = (f32[64,128]{1,0:T(8,128)S(1)}, f32[64,128]{1,0:T(8,128)S(1)}, u32[]{:S(2)}, u32[]{:S(2)}) collective-permute-start(f32[64,128]{1,0:T(8,128)S(1)} %get-tuple-element.59), channel_id=1, source_target_pairs={{4,0},{8,4},{12,8},{16,12},{20,16},{24,20},{28,24},{0,28},{5,1},{9... | collective-permute-start | bytes 98312 | tf_op jit(solution)/shard_map/ppermute | solution.py:237
  46.8 2.1 %collective-permute-done.9.from_low = f32[64,128]{1,0:T(8,128)S(1)} collective-permute-done((f32[64,128]{1,0:T(8,128)S(1)}, f32[64,128]{1,0:T(8,128)S(1)}, u32[]{:S(2)}, u32[]{:S(2)}) %collective-permute-start.9) | collective-permute-done | bytes 32800 | tf_op jit(solution)/shard_map/ppermute | solution.py:236
  48.9 1.3 %advance.7 = (bf16[128,1536]{1,0:T(8,128)(2,1)S(1)}, f32[64,256]{1,0:T(8,128)S(1)}, f32[64,128]{1,0:T(8,128)S(1)}, f32[64,128]{1,0:T(8,128)S(1)}) custom-call(s32[1]{0:T(128)S(6)} %copy.10.counts, bf16[128,1536]{1,0:T(8,128)(2,1)S(1)} %gather_local.8.local, f32[64,128]{1,0:T(8,128)S(1)} %collective-permute-done.9.from_low, ...), custom_call_target="tpu_custom_call" | custom-call | tf_op jit(solution)/shard_map/advance/pallas_call | solution.py:253
  50.2 0.8 %gather_local.9.local = bf16[128,1536]{1,0:T(8,128)(2,1)S(1)} custom-call(bf16[128,1536]{1,0:T(8,128)(2,1)S(1)} %get-tuple-element.62.table, s32[6,256]{1,0:T(8,128)S(1)} %copy-done), custom_call_target="tpu_custom_call" | custom-call | tf_op jit(solution)/shard_map/gather_local/pallas_call | solution.py:238
  51.0 1.9 %collective-permute-start.14 = (f32[64,256]{1,0:T(8,128)S(1)}, f32[64,256]{1,0:T(8,128)S(1)}, u32[]{:S(2)}, u32[]{:S(2)}) collective-permute-start(f32[64,256]{1,0:T(8,128)S(1)} %get-tuple-element.66), channel_id=1, source_target_pairs={{0,1},{1,2},{2,3},{4,5},{5,6},{6,7},{8,9},{9,10},{10,11},{12,13},{... | collective-permute-start | bytes 196616 | tf_op jit(solution)/shard_map/ppermute | solution.py:247
  53.0 4.7 %collective-permute-start.13 = (f32[64,128]{1,0:T(8,128)S(1)}, f32[64,128]{1,0:T(8,128)S(1)}, u32[]{:S(2)}, u32[]{:S(2)}) collective-permute-start(f32[64,128]{1,0:T(8,128)S(1)} %get-tuple-element.65), channel_id=1, source_target_pairs={{4,0},{8,4},{12,8},{16,12},{20,16},{24,20},{28,24},{0,28},{5,1},{9... | collective-permute-start | bytes 98312 | tf_op jit(solution)/shard_map/ppermute | solution.py:237
  57.7 1.9 %collective-permute-done.12.from_low = f32[64,128]{1,0:T(8,128)S(1)} collective-permute-done((f32[64,128]{1,0:T(8,128)S(1)}, f32[64,128]{1,0:T(8,128)S(1)}, u32[]{:S(2)}, u32[]{:S(2)}) %collective-permute-start.12) | collective-permute-done | bytes 32800 | tf_op jit(solution)/shard_map/ppermute | solution.py:236
  59.6 1.7 %advance_last.1 = f32[1,256,256]{2,1,0:T(8,128)} custom-call(s32[1]{0:T(128)S(6)} %copy.10.counts, bf16[128,1536]{1,0:T(8,128)(2,1)S(1)} %gather_local.9.local, f32[64,128]{1,0:T(8,128)S(1)} %collective-permute-done.12.from_low, f32[64,128]{1,0:T(8,128)S(1)} %collective-permute-done.13.from_high, f32[64,256]{1,0:T(8,128)S(1)} %collective-permute-done.14.top_in, ...), custom_call_target="tpu_custom_call" | custom-call | tf_op jit(solution)/shard_map/advance_last/pallas_call | solution.py:263
  (24 shorter events, 3.3 us)
Async XLA Ops:
  3.0 12.1 %copy-start.2 = (s32[256]{0:T(256)S(1)}, s32[256]{0:T(256)}, u32[]{:S(2)}) copy-start(s32[256]{0:T(256)} %param.16) | copy-start | bytes 3076
  3.0 0.7 %copy-start = (s32[6,256]{1,0:T(8,128)S(1)}, s32[6,256]{1,0:T(8,128)}, u32[]{:S(2)}) copy-start(s32[6,256]{1,0:T(8,128)} %links.19) | copy-start | bytes 18436
  3.7 11.4 %copy-start.1 = (s32[6,256]{1,0:T(8,128)S(1)}, s32[6,256]{1,0:T(8,128)}, u32[]{:S(2)}) copy-start(s32[6,256]{1,0:T(8,128)} %orient.9) | copy-start | bytes 18436
  4.5 10.6 %collective-permute-start.2 = (f32[64,256]{1,0:T(8,128)S(1)}, f32[64,256]{1,0:T(8,128)S(1)}, u32[]{:S(2)}, u32[]{:S(2)}) collective-permute-start(f32[64,256]{1,0:T(8,128)S(1)} %get-tuple-element.41), channel_id=1, source_target_pairs={{0,1},{1,2},{2,3},{4,5},{5,6},{6,7},{8,9},{9,10},{10,11},{12,13},{... | collective-permute-start | bytes 196616 | tf_op jit(solution)/shard_map/ppermute | solution.py:247
  6.9 8.2 %collective-permute-start = (f32[64,128]{1,0:T(8,128)S(1)}, f32[64,128]{1,0:T(8,128)S(1)}, u32[]{:S(2)}, u32[]{:S(2)}) collective-permute-start(f32[64,128]{1,0:T(8,128)S(1)} %get-tuple-element.39), channel_id=1, source_target_pairs={{0,4},{4,8},{8,12},{12,16},{16,20},{20,24},{24,28},{28,0},{1,5},{5... | collective-permute-start | bytes 98312 | tf_op jit(solution)/shard_map/ppermute | solution.py:236
  9.3 5.8 %collective-permute-start.1 = (f32[64,128]{1,0:T(8,128)S(1)}, f32[64,128]{1,0:T(8,128)S(1)}, u32[]{:S(2)}, u32[]{:S(2)}) collective-permute-start(f32[64,128]{1,0:T(8,128)S(1)} %get-tuple-element.40), channel_id=1, source_target_pairs={{4,0},{8,4},{12,8},{16,12},{20,16},{24,20},{28,24},{0,28},{5,1},{9... | collective-permute-start | bytes 98312 | tf_op jit(solution)/shard_map/ppermute | solution.py:237
  17.3 10.1 %collective-permute-start.5 = (f32[64,256]{1,0:T(8,128)S(1)}, f32[64,256]{1,0:T(8,128)S(1)}, u32[]{:S(2)}, u32[]{:S(2)}) collective-permute-start(f32[64,256]{1,0:T(8,128)S(1)} %get-tuple-element.48), channel_id=1, source_target_pairs={{0,1},{1,2},{2,3},{4,5},{5,6},{6,7},{8,9},{9,10},{10,11},{12,13},{... | collective-permute-start | bytes 196616 | tf_op jit(solution)/shard_map/ppermute | solution.py:247
  20.7 6.7 %collective-permute-start.3 = (f32[64,128]{1,0:T(8,128)S(1)}, f32[64,128]{1,0:T(8,128)S(1)}, u32[]{:S(2)}, u32[]{:S(2)}) collective-permute-start(f32[64,128]{1,0:T(8,128)S(1)} %get-tuple-element.46), channel_id=1, source_target_pairs={{0,4},{4,8},{8,12},{12,16},{16,20},{20,24},{24,28},{28,0},{1,5},{5... | collective-permute-start | bytes 98312 | tf_op jit(solution)/shard_map/ppermute | solution.py:236
  20.8 6.6 %collective-permute-start.4 = (f32[64,128]{1,0:T(8,128)S(1)}, f32[64,128]{1,0:T(8,128)S(1)}, u32[]{:S(2)}, u32[]{:S(2)}) collective-permute-start(f32[64,128]{1,0:T(8,128)S(1)} %get-tuple-element.47), channel_id=1, source_target_pairs={{4,0},{8,4},{12,8},{16,12},{20,16},{24,20},{28,24},{0,28},{5,1},{9... | collective-permute-start | bytes 98312 | tf_op jit(solution)/shard_map/ppermute | solution.py:237
  29.5 8.0 %collective-permute-start.8 = (f32[64,256]{1,0:T(8,128)S(1)}, f32[64,256]{1,0:T(8,128)S(1)}, u32[]{:S(2)}, u32[]{:S(2)}) collective-permute-start(f32[64,256]{1,0:T(8,128)S(1)} %get-tuple-element.54), channel_id=1, source_target_pairs={{0,1},{1,2},{2,3},{4,5},{5,6},{6,7},{8,9},{9,10},{10,11},{12,13},{... | collective-permute-start | bytes 196616 | tf_op jit(solution)/shard_map/ppermute | solution.py:247
  30.8 6.7 %collective-permute-start.6 = (f32[64,128]{1,0:T(8,128)S(1)}, f32[64,128]{1,0:T(8,128)S(1)}, u32[]{:S(2)}, u32[]{:S(2)}) collective-permute-start(f32[64,128]{1,0:T(8,128)S(1)} %get-tuple-element.52), channel_id=1, source_target_pairs={{0,4},{4,8},{8,12},{12,16},{16,20},{20,24},{24,28},{28,0},{1,5},{5... | collective-permute-start | bytes 98312 | tf_op jit(solution)/shard_map/ppermute | solution.py:236
  30.8 6.6 %collective-permute-start.7 = (f32[64,128]{1,0:T(8,128)S(1)}, f32[64,128]{1,0:T(8,128)S(1)}, u32[]{:S(2)}, u32[]{:S(2)}) collective-permute-start(f32[64,128]{1,0:T(8,128)S(1)} %get-tuple-element.53), channel_id=1, source_target_pairs={{4,0},{8,4},{12,8},{16,12},{20,16},{24,20},{28,24},{0,28},{5,1},{9... | collective-permute-start | bytes 98312 | tf_op jit(solution)/shard_map/ppermute | solution.py:237
  39.6 9.3 %collective-permute-start.11 = (f32[64,256]{1,0:T(8,128)S(1)}, f32[64,256]{1,0:T(8,128)S(1)}, u32[]{:S(2)}, u32[]{:S(2)}) collective-permute-start(f32[64,256]{1,0:T(8,128)S(1)} %get-tuple-element.60), channel_id=1, source_target_pairs={{0,1},{1,2},{2,3},{4,5},{5,6},{6,7},{8,9},{9,10},{10,11},{12,13},{... | collective-permute-start | bytes 196616 | tf_op jit(solution)/shard_map/ppermute | solution.py:247
  41.6 7.2 %collective-permute-start.9 = (f32[64,128]{1,0:T(8,128)S(1)}, f32[64,128]{1,0:T(8,128)S(1)}, u32[]{:S(2)}, u32[]{:S(2)}) collective-permute-start(f32[64,128]{1,0:T(8,128)S(1)} %get-tuple-element.58), channel_id=1, source_target_pairs={{0,4},{4,8},{8,12},{12,16},{16,20},{20,24},{24,28},{28,0},{1,5},{5... | collective-permute-start | bytes 98312 | tf_op jit(solution)/shard_map/ppermute | solution.py:236
  41.7 7.2 %collective-permute-start.10 = (f32[64,128]{1,0:T(8,128)S(1)}, f32[64,128]{1,0:T(8,128)S(1)}, u32[]{:S(2)}, u32[]{:S(2)}) collective-permute-start(f32[64,128]{1,0:T(8,128)S(1)} %get-tuple-element.59), channel_id=1, source_target_pairs={{4,0},{8,4},{12,8},{16,12},{20,16},{24,20},{28,24},{0,28},{5,1},{9... | collective-permute-start | bytes 98312 | tf_op jit(solution)/shard_map/ppermute | solution.py:237
  51.0 8.7 %collective-permute-start.14 = (f32[64,256]{1,0:T(8,128)S(1)}, f32[64,256]{1,0:T(8,128)S(1)}, u32[]{:S(2)}, u32[]{:S(2)}) collective-permute-start(f32[64,256]{1,0:T(8,128)S(1)} %get-tuple-element.66), channel_id=1, source_target_pairs={{0,1},{1,2},{2,3},{4,5},{5,6},{6,7},{8,9},{9,10},{10,11},{12,13},{... | collective-permute-start | bytes 196616 | tf_op jit(solution)/shard_map/ppermute | solution.py:247
  52.9 6.7 %collective-permute-start.12 = (f32[64,128]{1,0:T(8,128)S(1)}, f32[64,128]{1,0:T(8,128)S(1)}, u32[]{:S(2)}, u32[]{:S(2)}) collective-permute-start(f32[64,128]{1,0:T(8,128)S(1)} %get-tuple-element.64), channel_id=1, source_target_pairs={{0,4},{4,8},{8,12},{12,16},{16,20},{20,24},{24,28},{28,0},{1,5},{5... | collective-permute-start | bytes 98312 | tf_op jit(solution)/shard_map/ppermute | solution.py:236
  53.0 6.6 %collective-permute-start.13 = (f32[64,128]{1,0:T(8,128)S(1)}, f32[64,128]{1,0:T(8,128)S(1)}, u32[]{:S(2)}, u32[]{:S(2)}) collective-permute-start(f32[64,128]{1,0:T(8,128)S(1)} %get-tuple-element.65), channel_id=1, source_target_pairs={{4,0},{8,4},{12,8},{16,12},{20,16},{24,20},{28,24},{0,28},{5,1},{9... | collective-permute-start | bytes 98312 | tf_op jit(solution)/shard_map/ppermute | solution.py:237
